TPU v7x, 32 devices: a whole 2x2x4 slice. The times are simulated.
32 devices in a mesh: leaf: 32 (over z, y, x, core).
Axes of the slice: x: 2, y: 2, z: 4, core: 2. Of those that a mesh axis runs over, the one named last changes fastest.
Arguments:
- coords: float32 [3, 262144], P(None, 'leaf'), may hold values from 0 to 1
- charges: bfloat16 [262144, 128], P('leaf'), may hold values from -6 to 6
- near_leaves: int32 [2048, 27], P('leaf'), may hold values from 0 to 191
- leaf_basis: bfloat16 [2048, 4096], P('leaf'), may hold values from -1 to 1
- leaf_transfer: bfloat16 [2048, 1024], P('leaf'), may hold values from -0.75 to 0.75
- mid_transfer: bfloat16 [256, 1024], P('leaf'), may hold values from -0.75 to 0.75
- base_transfer: bfloat16 [32, 1024], P('leaf'), may hold values from -0.75 to 0.75
- base_coupling: bfloat16 [6048, 1024], P('leaf'), may hold values from -0.01953125 to 0.01953125
- base_target: int32 [6048, 1], P('leaf'), may hold values from 0 to 31; in each aligned block of 189 rows (0 to 188, 189 to 377, ...) at most 11 rows name the same one
- base_source: int32 [6048], P('leaf'), may hold values from 0 to 31
- top_coupling: bfloat16 [256, 1024], P('leaf'), may hold values from -0.015625 to 0.015625
- top_target: int32 [256], P('leaf'), may hold values from 0 to 3
- top_source: int32 [256], P('leaf'), may hold values from 0 to 3
Outputs:
- potential: bfloat16 [262144, 128], P('leaf')
Inputs may be any that keep to these rules, and one draw needn't show every extreme that they name: `near_leaves`: entry j of leaf l names leaf 64 * (l // 64 - 1) + j: a leaf of the device before in Morton order, of the row's own device, or of the device after; repeats may occur. `base_target`: among the 189 blocks of one device no base cluster is the target more than 11 times; that count is reached.
All inputs are finite; a program needn't handle non-finite values.
Results may differ from a plain program's by a relative error of at most 0.01.
Values may be sent and summed in bfloat16 or wider, within the bound.
A program may use at most 128 MiB of HBM per device.

v0:
```python
import functools
import math

import jax
import jax.numpy as jnp
from jax import lax
from jax.experimental import pallas as pl
from jax.experimental.pallas import tpu as pltpu
from jax.sharding import PartitionSpec as P

K = 32
RHS = 128
M = 128
FEATURES = 32
DELTA_SQ = 0.0025

F32 = jnp.float32
BF16 = jnp.bfloat16
VMEM = pl.BlockSpec(memory_space=pltpu.VMEM)
SMEM = pl.BlockSpec(memory_space=pltpu.SMEM)
ANY = pl.BlockSpec(memory_space=pl.ANY)


def dot(a, b):
    return jnp.dot(a, b, preferred_element_type=F32)


def dot_ta(a, b):
    return lax.dot_general(a, b, (((0,), (0,)), ((), ())), preferred_element_type=F32)


def rows(index, size):
    return pl.ds(pl.multiple_of(index * size, size), size)


def pieces(x):
    high = x.astype(BF16).astype(F32)
    rest = x - high
    middle = rest.astype(BF16).astype(F32)
    return high, middle, (rest - middle).astype(BF16).astype(F32)


def write_features(rows_ref, first, width, parts):
    at = 0
    for part in parts:
        rows_ref[at : at + part.shape[0], pl.ds(first, width)] = part
        at += part.shape[0]


def up_kernel(leaves, basis_ref, charges_ref, leaf_t_ref, mid_t_ref, base_t_ref, out_ref, coeffs):
    def group(i, carry):
        for j in range(8):
            leaf = i * 8 + j
            coeffs[rows(leaf, K), :] = dot(
                basis_ref[rows(leaf, K), :], charges_ref[rows(leaf, M), :]
            ).astype(BF16)
        return carry

    lax.fori_loop(0, leaves // 8, group, 0)
    mids = []
    for m in range(leaves // 8):
        part = slice(m * 8 * K, (m + 1) * 8 * K)
        mids.append(dot_ta(leaf_t_ref[part, :], coeffs[part, :]).astype(BF16))
    base = dot_ta(mid_t_ref[...], jnp.concatenate(mids, axis=0)).astype(BF16)
    out_ref[:K, :] = base
    out_ref[K:, :] = dot_ta(base_t_ref[...], base).astype(BF16)


def couple_kernel(
    devices, blocks, top_blocks, step,
    target_ref, source_ref, top_target_ref, top_source_ref,
    blocks_ref, top_blocks_ref, all_ref, out_ref, sums, top_coeffs, top_sums,
):
    sums[...] = jnp.zeros_like(sums)
    top_sums[...] = jnp.zeros_like(top_sums)
    for t in range(devices // 8):
        total = jnp.zeros((K, RHS), F32)
        for j in range(8):
            first = (t * 8 + j) * 2 * K + K
            total = total + all_ref[first : first + K, :].astype(F32)
        top_coeffs[t * K : (t + 1) * K, :] = total.astype(BF16)

    def group(i, carry):
        products = []
        for j in range(step):
            b = i * step + j
            products.append(
                dot(blocks_ref[rows(b, K), :], all_ref[rows(source_ref[b] * 2, K), :])
            )
        for j in range(step):
            where = rows(target_ref[i * step + j], K)
            sums[where, :] = sums[where, :] + products[j]
        return carry

    lax.fori_loop(0, blocks // step, group, 0)
    products = [
        dot(top_blocks_ref[b * K : (b + 1) * K, :], top_coeffs[rows(top_source_ref[b], K), :])
        for b in range(top_blocks)
    ]
    for b in range(top_blocks):
        where = rows(top_target_ref[b], K)
        top_sums[where, :] = top_sums[where, :] + products[b]
    for d in range(devices):
        out_ref[d * 2 * K : d * 2 * K + K, :] = sums[d * K : (d + 1) * K, :].astype(BF16)
        t = d // 8
        out_ref[d * 2 * K + K : (d + 1) * 2 * K, :] = top_sums[t * K : (t + 1) * K, :].astype(BF16)


def groups_of(named):
    return [range(j, min(j + 2, named)) for j in range(0, named, 2)]


def make_kernel(
    leaves, named, scale, width,
    near_ref, before_ref, own_ref, after_ref, out_ref, targets, staged, sources,
):
    points = leaves * M

    @pl.when(pl.program_id(0) == 0)
    def _():
        for place, ref in enumerate((before_ref, own_ref, after_ref)):

            def chunk(i, carry, place=place, ref=ref):
                first = pl.multiple_of(i * width, width)
                x = (ref[:, pl.ds(first, width)] - 0.5) * scale
                h, m, l = pieces(x)
                norm = x[0:1] * x[0:1] + x[1:2] * x[1:2] + x[2:3] * x[2:3]
                ones = jnp.ones((3, width), F32)
                zeros = jnp.zeros((FEATURES - 24, width), F32)
                if place == 1:
                    n = pieces(norm + DELTA_SQ * scale * scale)
                    write_features(targets, first, width, [h, h, m, h, l, m, *n, ones, zeros])
                n = pieces(norm)
                h, m, l = -2.0 * h, -2.0 * m, -2.0 * l
                write_features(staged, 0, width, [h, m, h, l, h, m, ones, *n, zeros])
                where = pl.ds(pl.multiple_of(place * points + first, width), width)
                sources[:, where] = staged[...].astype(BF16)
                return carry

            lax.fori_loop(0, points // width, chunk, 0)

    for k in range(out_ref.shape[0]):
        leaf = pl.program_id(0) * out_ref.shape[0] + k
        mine = targets[:, rows(leaf, M)].T.astype(BF16)
        for group in groups_of(named):
            theirs = jnp.concatenate(
                [sources[:, rows(near_ref[leaf, j], M)] for j in group], axis=1
            )
            squares = dot(mine, theirs)
            out_ref[k, :, group[0] * M : (group[-1] + 1) * M] = lax.rsqrt(squares.astype(BF16))


def use_kernel(
    devices, leaves, named,
    near_ref, kernel_ref, before_ref, own_ref, after_ref, got_ref,
    basis_ref, leaf_t_ref, mid_t_ref, base_t_ref, out_ref,
    pool, fields, sems,
):
    points = leaves * M

    @pl.when(pl.program_id(0) == 0)
    def _():
        copies = [
            pltpu.make_async_copy(ref, pool.at[pl.ds(i * points, points), :], sems.at[i])
            for i, ref in enumerate((before_ref, own_ref, after_ref))
        ]
        for copy in copies:
            copy.start()
        total = jnp.sum(got_ref[...].astype(F32).reshape(devices, 2 * K, RHS), axis=0)
        base = (total[:K] + dot(base_t_ref[...], total[K:].astype(BF16))).astype(BF16)
        mid = dot(mid_t_ref[...], base).astype(BF16)
        for m in range(leaves // 8):
            part = slice(m * 8 * K, (m + 1) * 8 * K)
            fields[part, :] = dot(leaf_t_ref[part, :], mid[m * K : (m + 1) * K, :]).astype(BF16)
        for copy in copies:
            copy.wait()

    for k in range(kernel_ref.shape[0]):
        leaf = pl.program_id(0) * kernel_ref.shape[0] + k
        total = dot_ta(basis_ref[rows(leaf, K), :], fields[rows(leaf, K), :])
        for group in groups_of(named):
            theirs = jnp.concatenate([pool[rows(near_ref[leaf, j], M), :] for j in group], axis=0)
            total = total + dot(kernel_ref[k, :, group[0] * M : (group[-1] + 1) * M], theirs)
        out_ref[k * M : (k + 1) * M, :] = total.astype(BF16)


def per_device(
    coords,
    charges,
    near_leaves,
    leaf_basis,
    leaf_transfer,
    mid_transfer,
    base_transfer,
    base_coupling,
    base_target,
    base_source,
    top_coupling,
    top_target,
    top_source,
):
    leaves, named = near_leaves.shape
    devices = lax.axis_size("leaf")
    blocks, top_blocks = base_coupling.shape[0], top_coupling.shape[0]
    scale = math.sqrt(named * M)
    up = [(i, i + 1) for i in range(devices - 1)]
    down = [(i + 1, i) for i in range(devices - 1)]
    points_before = lax.ppermute(coords, "leaf", up)
    points_after = lax.ppermute(coords, "leaf", down)

    basis = leaf_basis.reshape(-1, M)
    leaf_t = leaf_transfer.reshape(-1, K)
    mid_t = mid_transfer.reshape(-1, K)
    base_t = base_transfer.reshape(-1, K)
    limit = pltpu.CompilerParams(vmem_limit_bytes=48 * 1024 * 1024)

    mine = pl.pallas_call(
        functools.partial(up_kernel, leaves),
        out_shape=jax.ShapeDtypeStruct((2 * K, RHS), BF16),
        in_specs=[VMEM] * 5,
        out_specs=VMEM,
        scratch_shapes=[pltpu.VMEM((leaves * K, RHS), BF16)],
        compiler_params=limit,
        cost_estimate=pl.CostEstimate(flops=70_000_000, bytes_accessed=3_000_000, transcendentals=0),
        name="upward",
    )(basis, charges, leaf_t, mid_t, base_t)
    gathered = lax.all_gather(mine, "leaf", axis=0, tiled=True)
    gathered, outgoing, points_before, points_after = lax.optimization_barrier(
        (gathered, charges, points_before, points_after)
    )
    charges_before = lax.ppermute(outgoing, "leaf", up)
    charges_after = lax.ppermute(outgoing, "leaf", down)

    step = max(s for s in range(1, 33) if blocks % s == 0)
    partial = pl.pallas_call(
        functools.partial(couple_kernel, devices, blocks, top_blocks, step),
        out_shape=jax.ShapeDtypeStruct((devices * 2 * K, RHS), BF16),
        in_specs=[SMEM] * 4 + [VMEM] * 3,
        out_specs=VMEM,
        scratch_shapes=[
            pltpu.VMEM((devices * K, RHS), F32),
            pltpu.VMEM((devices // 8 * K, RHS), BF16),
            pltpu.VMEM((devices // 8 * K, RHS), F32),
        ],
        compiler_params=limit,
        cost_estimate=pl.CostEstimate(flops=50_000_000, bytes_accessed=3_000_000, transcendentals=0),
        name="couple",
    )(
        base_target[:, 0], base_source, top_target, top_source,
        base_coupling.reshape(-1, K), top_coupling.reshape(-1, K), gathered,
    )
    got = lax.all_to_all(partial, "leaf", split_axis=0, concat_axis=0, tiled=True)

    partial, points_before = lax.optimization_barrier((partial, points_before))
    got = lax.all_to_all(partial, "leaf", split_axis=0, concat_axis=0, tiled=True)
    each = 4
    kernels = pl.pallas_call(
        functools.partial(make_kernel, leaves, named, scale, 1024),
        grid=(leaves // each,),
        out_shape=jax.ShapeDtypeStruct((leaves, M, named * M), BF16),
        in_specs=[SMEM, VMEM, VMEM, VMEM],
        out_specs=pl.BlockSpec((each, M, named * M), lambda i: (i, 0, 0)),
        scratch_shapes=[
            pltpu.VMEM((FEATURES, leaves * M), F32),
            pltpu.VMEM((FEATURES, 1024), F32),
            pltpu.VMEM((FEATURES, 3 * leaves * M), BF16),
        ],
        compiler_params=limit,
        cost_estimate=pl.CostEstimate(
            flops=16_000_000_000, bytes_accessed=60_000_000, transcendentals=28_000_000
        ),
        name="make",
    )(near_leaves, points_before, coords, points_after)
    return pl.pallas_call(
        functools.partial(use_kernel, devices, leaves, named),
        grid=(leaves // each,),
        out_shape=jax.ShapeDtypeStruct((leaves * M, RHS), BF16),
        in_specs=[SMEM, pl.BlockSpec((each, M, named * M), lambda i: (i, 0, 0)), ANY, ANY, ANY]
        + [VMEM] * 5,
        out_specs=pl.BlockSpec((each * M, RHS), lambda i: (i, 0)),
        scratch_shapes=[
            pltpu.VMEM((3 * leaves * M, RHS), BF16),
            pltpu.VMEM((leaves * K, RHS), BF16),
            pltpu.SemaphoreType.DMA((3,)),
        ],
        compiler_params=limit,
        cost_estimate=pl.CostEstimate(
            flops=8_000_000_000, bytes_accessed=66_000_000, transcendentals=0
        ),
        name="use",
    )(
        near_leaves, kernels, charges_before, charges, charges_after, got,
        basis, leaf_t, mid_t, base_t,
    )


def solution(mesh):
    split, flat = P("leaf", None), P("leaf")
    in_specs = (P(None, "leaf"),) + (split,) * 8 + (flat, split, flat, flat)
    return jax.shard_map(
        per_device, mesh=mesh, in_specs=in_specs, out_specs=split, check_vma=False
    )
```

profile of v0, /device:TPU:0, one launch (start us, length us, event | category | flops | bytes accessed | tf_op | source)
XLA Modules:
  0.0 146.8 jit_solution(18217806694936892634)
XLA Ops:
  0.0 2.4 %collective-permute-start = (f32[3,8192]{1,0:T(4,128)}, f32[3,8192]{1,0:T(4,128)S(1)}, u32[]{:S(2)}, u32[]{:S(2)}) collective-permute-start(f32[3,8192]{1,0:T(4,128)} %own_ref.2), channel_id=1, source_target_pairs={{0,1},{1,2},{2,3},{3,4},{4,5},{5,6},{6,7},{7,8},{8,9},{9,10},{10,1... | collective-permute-start | bytes 294920 | tf_op jit(solution)/shard_map/ppermute | solution.py:208
  2.4 1.3 collective-permute-start.1
  3.7 0.7 reduce
  4.4 0.1 reshape.25.base_t_ref
  4.5 0.8 reshape.24.mid_t_ref
  5.3 1.3 reshape.22.basis_ref
  6.6 0.0 copy-start.10
  6.6 0.0 copy-start.11
  6.7 1.3 reshape.23.leaf_t_ref
  8.0 3.6 %upward.1 = bf16[64,128]{1,0:T(8,128)(2,1)S(1)} custom-call(bf16[2048,128]{1,0:T(8,128)(2,1)S(1)} %reshape.22.basis_ref, bf16[8192,128]{1,0:T(8,128)(2,1)} %own_ref.3, bf16[2048,32]{1,0:T(8,128)(2,1)S(1)} %reshape.23.leaf_t_ref, bf16[256,32]{1,0:T(8,128)(2,1)S(1)} %reshape.24.mid_t_ref, bf16[32,32]{1,0:T(8,128)(2,1)S(1)} %reshape.25.base_t_ref), custom_call_target="tpu_custom_call" | custom-call | flops 70000000 | bytes 3000000 | tf_op jit(solution)/shard_map/upward/pallas_call | solution.py:217
  11.5 0.0 copy-start.3
  11.6 0.0 copy-start.4
  11.6 46.7 %all_gather.3.all_ref = bf16[2048,128]{1,0:T(8,128)(2,1)S(1)} all-gather(bf16[64,128]{1,0:T(8,128)(2,1)S(1)} %upward.1), channel_id=1, replica_groups=mesh['leaf'=32] {'leaf'}, dimensions={0}, use_global_device_ids=true | all-gather | bytes 540672 | tf_op jit(solution)/shard_map/all_gather | solution.py:227
  58.2 0.0 collective-permute-done.before_ref
  58.2 0.7 copy-done.6
  58.9 0.0 collective-permute-done.1.after_ref
  58.9 0.6 copy-done.8
  59.6 1.3 collective-permute-start.3
  60.8 4.4 %collective-permute-start.2 = (bf16[8192,128]{1,0:T(8,128)(2,1)}, bf16[8192,128]{1,0:T(8,128)(2,1)}, u32[]{:S(2)}, u32[]{:S(2)}) collective-permute-start(bf16[8192,128]{1,0:T(8,128)(2,1)} %own_ref.3), channel_id=1, source_target_pairs={{0,1},{1,2},{2,3},{3,4},{4,5},{5,6},{6,7},{7,8},{8,9},{9,10},{10,1... | collective-permute-start | bytes 6291464 | tf_op jit(solution)/shard_map/ppermute | solution.py:231
  65.2 0.1 copy.17.near_ref
  65.3 0.1 reshape.21.top_blocks_ref
  65.4 2.2 %reshape.20.blocks_ref = bf16[6048,32]{1,0:T(8,128)(2,1)S(1)} reshape(bf16[189,1024]{1,0:T(8,128)(2,1)} %param.20) | data formatting | bytes 774144 | tf_op jit(solution)/shard_map/reshape | solution.py:250
  67.7 0.0 copy-start.5
  67.7 2.7 %couple.1 = bf16[2048,128]{1,0:T(8,128)(2,1)S(1)} custom-call(s32[189]{0:T(256)S(1)} %bitcast.5, s32[189]{0:T(256)S(1)} %copy-done.2, s32[8]{0:T(128)S(1)} %copy-done.3, s32[8]{0:T(128)S(1)} %copy-done.4, bf16[6048,32]{1,0:T(8,128)(2,1)S(1)} %reshape.20.blocks_ref, bf16[256,32]{1,0:T(8,128)(2,1)S(1)} %reshape.21.top_blocks_ref, ...), custom_call_target="tpu_custom_call" | custom-call | flops 50000000 | bytes 3000000 | tf_op jit(solution)/shard_map/couple/pallas_call | solution.py:235
  70.4 0.0 copy-start
  70.4 0.8 copy-done
  71.2 2.6 %all-to-all-start = ((bf16[32,64,128]{2,1,0:T(8,128)(2,1)}), bf16[32,64,128]{2,1,0:T(8,128)(2,1)S(1)}, u32[]{:S(2)}, u32[]{:S(2)}) async-start(bf16[32,64,128]{2,1,0:T(8,128)(2,1)} %bitcast.4), calls=%async_computation | async-start | bytes 1048576 | tf_op jit(solution)/shard_map/all_to_all | solution.py:255
  73.8 0.9 copy-done.7
  74.7 0.9 copy-done.9
  75.6 27.4 %make.1.kernel_ref = bf16[64,128,3456]{2,1,0:T(8,128)(2,1)} custom-call(s32[64,27]{1,0:T(8,128)S(1)} %copy.17.near_ref, f32[3,8192]{1,0:T(4,128)S(1)} %copy-done.7, f32[3,8192]{1,0:T(4,128)S(1)} %copy-done.5, f32[3,8192]{1,0:T(4,128)S(1)} %copy-done.9), custom_call_target="tpu_custom_call" | custom-call | flops 16000000000 | bytes 60000000 | tf_op jit(solution)/shard_map/make/pallas_call | solution.py:257
  103.0 11.8 %all-to-all-done = bf16[32,64,128]{2,1,0:T(8,128)(2,1)S(1)} async-done(((bf16[32,64,128]{2,1,0:T(8,128)(2,1)}), bf16[32,64,128]{2,1,0:T(8,128)(2,1)S(1)}, u32[]{:S(2)}, u32[]{:S(2)}) %all-to-all-start) | async-done | bytes 524320 | tf_op jit(solution)/shard_map/all_to_all | solution.py:255
  114.9 31.9 %use.1 = bf16[8192,128]{1,0:T(8,128)(2,1)} custom-call(s32[64,27]{1,0:T(8,128)S(1)} %copy.17.near_ref, bf16[64,128,3456]{2,1,0:T(8,128)(2,1)} %make.1.kernel_ref, bf16[8192,128]{1,0:T(8,128)(2,1)} %collective-permute-done.2.before_ref, bf16[8192,128]{1,0:T(8,128)(2,1)} %own_ref.3, bf16[8192,128]{1,0:T(8,128)(2,1)} %collective-permute-done.3.after_ref, ...), custom_call_target="tpu_custom_call" | custom-call | flops 8000000000 | bytes 66000000 | tf_op jit(solution)/shard_map/use/pallas_call | solution.py:274
  (15 shorter events, 0.0 us)
Async XLA Ops:
  0.0 58.2 %collective-permute-start = (f32[3,8192]{1,0:T(4,128)}, f32[3,8192]{1,0:T(4,128)S(1)}, u32[]{:S(2)}, u32[]{:S(2)}) collective-permute-start(f32[3,8192]{1,0:T(4,128)} %own_ref.2), channel_id=1, source_target_pairs={{0,1},{1,2},{2,3},{3,4},{4,5},{5,6},{6,7},{7,8},{8,9},{9,10},{10,1... | collective-permute-start | bytes 294920 | tf_op jit(solution)/shard_map/ppermute | solution.py:208
  2.4 56.5 %collective-permute-start.1 = (f32[3,8192]{1,0:T(4,128)}, f32[3,8192]{1,0:T(4,128)S(1)}, u32[]{:S(2)}, u32[]{:S(2)}) collective-permute-start(f32[3,8192]{1,0:T(4,128)} %own_ref.2), channel_id=1, source_target_pairs={{1,0},{2,1},{3,2},{4,3},{5,4},{6,5},{7,6},{8,7},{9,8},{10,9},{11,1... | collective-permute-start | bytes 294920 | tf_op jit(solution)/shard_map/ppermute | solution.py:209
  6.6 58.6 %copy-start.10 = (s32[64,27]{0,1:T(8,128)S(1)}, s32[64,27]{0,1:T(8,128)}, u32[]{:S(2)}) copy-start(s32[64,27]{0,1:T(8,128)} %param.15) | copy-start | bytes 20740
  6.6 58.7 %copy-start.11 = (bf16[8,1024]{1,0:T(8,128)(2,1)S(1)}, bf16[8,1024]{1,0:T(8,128)(2,1)}, u32[]{:S(2)}) copy-start(bf16[8,1024]{1,0:T(8,128)(2,1)} %param.23) | copy-start | bytes 49156
  11.5 56.2 %copy-start.1 = (s32[189,1]{0,1:T(1,128)S(1)}, s32[189,1]{0,1:T(1,128)}, u32[]{:S(2)}) copy-start(s32[189,1]{0,1:T(1,128)} %param.21) | copy-start | bytes 2272
  11.5 56.2 %copy-start.2 = (s32[189]{0:T(256)S(1)}, s32[189]{0:T(256)}, u32[]{:S(2)}) copy-start(s32[189]{0:T(256)} %source_ref.1) | copy-start | bytes 2272
  11.5 56.2 %copy-start.3 = (s32[8]{0:T(128)S(1)}, s32[8]{0:T(128)}, u32[]{:S(2)}) copy-start(s32[8]{0:T(128)} %top_target_ref.1) | copy-start | bytes 100
  11.6 56.2 %copy-start.4 = (s32[8]{0:T(128)S(1)}, s32[8]{0:T(128)}, u32[]{:S(2)}) copy-start(s32[8]{0:T(128)} %top_source_ref.1) | copy-start | bytes 100
  58.2 0.7 copy-start.6
  58.9 0.7 copy-start.8
  59.6 55.3 %collective-permute-start.3 = (bf16[8192,128]{1,0:T(8,128)(2,1)}, bf16[8192,128]{1,0:T(8,128)(2,1)}, u32[]{:S(2)}, u32[]{:S(2)}) collective-permute-start(bf16[8192,128]{1,0:T(8,128)(2,1)} %own_ref.3), channel_id=1, source_target_pairs={{1,0},{2,1},{3,2},{4,3},{5,4},{6,5},{7,6},{8,7},{9,8},{10,9},{11,1... | collective-permute-start | bytes 6291464 | tf_op jit(solution)/shard_map/ppermute | solution.py:232
  60.8 54.0 %collective-permute-start.2 = (bf16[8192,128]{1,0:T(8,128)(2,1)}, bf16[8192,128]{1,0:T(8,128)(2,1)}, u32[]{:S(2)}, u32[]{:S(2)}) collective-permute-start(bf16[8192,128]{1,0:T(8,128)(2,1)} %own_ref.3), channel_id=1, source_target_pairs={{0,1},{1,2},{2,3},{3,4},{4,5},{5,6},{6,7},{7,8},{8,9},{9,10},{10,1... | collective-permute-start | bytes 6291464 | tf_op jit(solution)/shard_map/ppermute | solution.py:231
  67.7 6.1 %copy-start.5 = (f32[3,8192]{1,0:T(4,128)S(1)}, f32[3,8192]{1,0:T(4,128)}, u32[]{:S(2)}) copy-start(f32[3,8192]{1,0:T(4,128)} %own_ref.2) | copy-start | bytes 294916
  70.4 0.8 copy-start
  71.2 43.7 %all-to-all-start = ((bf16[32,64,128]{2,1,0:T(8,128)(2,1)}), bf16[32,64,128]{2,1,0:T(8,128)(2,1)S(1)}, u32[]{:S(2)}, u32[]{:S(2)}) async-start(bf16[32,64,128]{2,1,0:T(8,128)(2,1)} %bitcast.4), calls=%async_computation | async-start | bytes 1048576 | tf_op jit(solution)/shard_map/all_to_all | solution.py:255
  73.8 0.9 copy-start.7
  74.7 0.9 copy-start.9
where the time goes:
time: 148 us; the launch traced here: 147 us
  Pallas kernels  65.5 us (44%)
  blocking collectives  46.7 us (32%)
  starting transfers between devices  12 us (8%)
  waiting for transfers between devices  11.9 us (8%)
  local copies, waits for them, and re-layouts  9.88 us (7%)
    all_gather x1, blocking collectives, per_device(): gathered = lax.all_gather(mine, 'leaf', axis=0, tiled=True)  46.7 us
    pallas_call x1, Pallas kernels, per_device(): pl.pallas_call(functools.partial(use_kernel, devices, leaves, named), gri...  31.9 us
    pallas_call x1, Pallas kernels, per_device(): pl.pallas_call(functools.partial(make_kernel, leaves, named, scale, 1024)...  27.4 us
    all_to_all x1, waiting for transfers between devices, per_device(): lax.all_to_all(partial, 'leaf', split_axis=0, concat_axis=0, tiled=True)  11.8 us
    ppermute x1, starting transfers between devices, per_device(): charges_before = lax.ppermute(outgoing, 'leaf', up)  4.38 us
    unnamed x25, local copies, waits for them, and re-layouts  4.04 us
    pallas_call x1, Pallas kernels, per_device(): pl.pallas_call(functools.partial(up_kernel, leaves), out_shape=jax.ShapeD...  3.56 us
  transfers between devices with their start and end apart: 5, of which 1 were waited for; matrix products, arithmetic and copies ran while one was open for 5% of the time, Pallas kernels for 23%

commit v1 on v0

v1 whole, which is shorter than its diff:
```python
import functools
import math

import jax
import jax.numpy as jnp
from jax import lax
from jax.experimental import pallas as pl
from jax.experimental.pallas import tpu as pltpu
from jax.sharding import PartitionSpec as P

K = 32
RHS = 128
M = 128
FEATURES = 32
DELTA_SQ = 0.0025
CHUNKS = 16
EACH = 2
WIDTH = 1024

F32 = jnp.float32
BF16 = jnp.bfloat16
MESH = pl.DeviceIdType.MESH
VMEM = pl.BlockSpec(memory_space=pltpu.VMEM)
SMEM = pl.BlockSpec(memory_space=pltpu.SMEM)
ANY = pl.BlockSpec(memory_space=pl.ANY)


def dot(a, b):
    return jnp.dot(a, b, preferred_element_type=F32)


def dot_ta(a, b):
    return lax.dot_general(a, b, (((0,), (0,)), ((), ())), preferred_element_type=F32)


def rows(index, size):
    return pl.ds(pl.multiple_of(index * size, size), size)


def pieces(x):
    high = x.astype(BF16).astype(F32)
    rest = x - high
    middle = rest.astype(BF16).astype(F32)
    return high, middle, (rest - middle).astype(BF16).astype(F32)


def write_features(rows_ref, first, width, parts):
    at = 0
    for part in parts:
        rows_ref[at : at + part.shape[0], pl.ds(first, width)] = part
        at += part.shape[0]


def groups_of(named):
    return [range(j, min(j + 2, named)) for j in range(0, named, 2)]


def levels_of(devices):
    half = devices // 2
    low = 2 ** (int(math.log2(half // 4)) // 2)
    levels, stride = [], 1
    for size in (low, half // 4 // low, 4):
        levels.append((stride, size))
        stride *= size
    return levels


def exchange_kernel(
    devices, leaves, named, blocks, top_blocks, step, scale,
    near_ref, source_ref, top_source_ref,
    coords_ref, charges_ref,
    top_target_ref, target_ref, basis_ref, leaf_t_ref, mid_t_ref, base_t_ref, blocks_ref, top_blocks_ref,
    kernels_ref, before_ref, after_ref, fields_ref,
    points, own, features, targets, staged, made, coeffs, gathered,
    products, partial, core_got, top_coeffs, *rest,
):
    levels = levels_of(devices)
    currents, receives = rest[: len(levels)], rest[len(levels) : 2 * len(levels)]
    (local_sem, made_sem, point_send, point_recv, up_send, down_send, near_recv,
     gather_send, gather_recv, reduce_send, reduce_recv) = rest[2 * len(levels) :]
    count = leaves * M
    part = count // CHUNKS
    half = devices // 2
    me = lax.axis_index("leaf")
    core, place = me % 2, me // 2
    has_before, has_after = me > 0, me < devices - 1
    twin = place * 2 + (1 - core)

    own_copy = pltpu.make_async_copy(charges_ref, own, local_sem.at[0])
    own_points = pltpu.make_async_copy(coords_ref, points.at[1], local_sem.at[1])
    own_points.start()
    own_copy.start()

    def digit(stride, size):
        return (place // stride) % size

    def peer(stride, size, turn):
        mine = digit(stride, size)
        other = (mine + turn) % size
        return other, (place + (other - mine) * stride) * 2 + core

    barrier = pltpu.get_barrier_semaphore()
    met = 1
    pl.semaphore_signal(barrier, inc=1, device_id=(twin,), device_id_type=MESH)
    for stride, size in levels:
        for turn in range(1, size):
            met += 1
            pl.semaphore_signal(
                barrier, inc=1, device_id=(peer(stride, size, turn)[1],), device_id_type=MESH
            )

    @pl.when(has_before)
    def _():
        pl.semaphore_signal(barrier, inc=1, device_id=(me - 1,), device_id_type=MESH)

    @pl.when(has_after)
    def _():
        pl.semaphore_signal(barrier, inc=1, device_id=(me + 1,), device_id_type=MESH)

    pl.semaphore_wait(
        barrier, met + jnp.where(has_before, 1, 0) + jnp.where(has_after, 1, 0)
    )

    def remote(src, dst, send, recv, device):
        return pltpu.make_async_remote_copy(
            src_ref=src, dst_ref=dst, send_sem=send, recv_sem=recv,
            device_id=(device,), device_id_type=MESH,
        )

    def points_up():
        return remote(coords_ref, points.at[0], point_send.at[0], point_recv.at[0], me + 1)

    def points_down():
        return remote(coords_ref, points.at[2], point_send.at[1], point_recv.at[1], me - 1)

    def chunk_up(c):
        return remote(
            charges_ref.at[rows(c, part), :], before_ref.at[rows(c, part), :],
            up_send.at[c], near_recv.at[0], me + 1,
        )

    def chunk_down(c):
        return remote(
            charges_ref.at[rows(c, part), :], after_ref.at[rows(c, part), :],
            down_send.at[c], near_recv.at[1], me - 1,
        )

    def send_chunk(c):
        @pl.when(has_after)
        def _():
            chunk_up(c).start()

        @pl.when(has_before)
        def _():
            chunk_down(c).start()

    @pl.when(has_after)
    def _():
        points_up().start()

    @pl.when(has_before)
    def _():
        points_down().start()

    @pl.when(jnp.logical_not(has_before))
    def _():
        points[0] = jnp.zeros((3, count), F32)

    @pl.when(jnp.logical_not(has_after))
    def _():
        points[2] = jnp.zeros((3, count), F32)

    send_chunk(0)
    send_chunk(1)

    own_copy.wait()

    def up_group(i, carry):
        for j in range(8):
            leaf = i * 8 + j
            coeffs[rows(leaf, K), :] = dot(
                basis_ref[rows(leaf, K), :], own[rows(leaf, M), :]
            ).astype(BF16)
        return carry

    lax.fori_loop(0, leaves // 8, up_group, 0)
    mids = []
    for m in range(leaves // 8):
        area = slice(m * 8 * K, (m + 1) * 8 * K)
        mids.append(dot_ta(leaf_t_ref[area, :], coeffs[area, :]).astype(BF16))
    base = dot_ta(mid_t_ref[...], jnp.concatenate(mids, axis=0)).astype(BF16)
    spot = core * half + place
    gathered[spot] = jnp.concatenate(
        [base, dot_ta(base_t_ref[...], base).astype(BF16)], axis=0
    )

    def featured(which):
        def chunk(i, carry):
            first = pl.multiple_of(i * WIDTH, WIDTH)
            x = (points[which, :, pl.ds(first, WIDTH)] - 0.5) * scale
            h, m, l = pieces(x)
            norm = x[0:1] * x[0:1] + x[1:2] * x[1:2] + x[2:3] * x[2:3]
            ones = jnp.ones((3, WIDTH), F32)
            zeros = jnp.zeros((FEATURES - 24, WIDTH), F32)
            if which == 1:
                n = pieces(norm + DELTA_SQ * scale * scale)
                write_features(targets, first, WIDTH, [h, h, m, h, l, m, *n, ones, zeros])
            n = pieces(norm)
            h, m, l = -2.0 * h, -2.0 * m, -2.0 * l
            write_features(staged, 0, WIDTH, [h, m, h, l, h, m, ones, *n, zeros])
            for k in range(WIDTH // M):
                features[which * leaves + i * (WIDTH // M) + k] = staged[
                    :, k * M : (k + 1) * M
                ].astype(BF16)
            return carry

        lax.fori_loop(0, count // WIDTH, chunk, 0)

    def gather_copies(level):
        if level == len(levels):
            where = rows(core, half)
            return [remote(
                gathered.at[where], gathered.at[where],
                gather_send.at[level, 0], gather_recv.at[level, 0], twin,
            )]
        stride, size = levels[level]
        copies = []
        for turn in range(1, size):
            where = rows((core * half + place) // stride, stride)
            copies.append(remote(
                gathered.at[where], gathered.at[where],
                gather_send.at[level, turn - 1], gather_recv.at[level, turn - 1],
                peer(stride, size, turn)[1],
            ))
        return copies

    def reduce_copies(level):
        if level == len(levels):
            return [remote(
                partial.at[rows(1 - core, half * 2 * K), :], core_got,
                reduce_send.at[level, 0], reduce_recv.at[level, 0], twin,
            )]
        stride, size = levels[level]
        copies = []
        for turn in range(1, size):
            other, device = peer(stride, size, turn)
            copies.append(remote(
                currents[level].at[rows(other, stride * 2 * K), :], receives[level].at[turn - 1],
                reduce_send.at[level, turn - 1], reduce_recv.at[level, turn - 1], device,
            ))
        return copies

    def start(copies):
        for copy in copies:
            copy.start()

    def arrived(copies):
        for copy in copies:
            copy.wait_recv()

    def sent(copies):
        for copy in copies:
            copy.wait_send()

    def spot_of(device):
        return (device % 2) * half + device // 2

    def couple():
        for t in range(devices // 8):
            total = jnp.zeros((K, RHS), F32)
            for j in range(8):
                total = total + gathered[spot_of(t * 8 + j), K:, :].astype(F32)
            top_coeffs[t] = total.astype(BF16)

        def group(i, carry):
            for j in range(step):
                b = i * step + j
                source = source_ref[b]
                where = (source & 1) * half + (source >> 1)
                products[rows(b, K), :] = dot(
                    blocks_ref[rows(b, K), :], gathered[where, :K, :]
                )
            return carry

        lax.fori_loop(0, blocks // step, group, 0)
        named_spot = target_ref[...]
        named_spot = (named_spot & 1) * half + (named_spot >> 1)
        ids = lax.broadcasted_iota(jnp.int32, (devices, blocks), 0)
        chosen = jnp.where(ids == named_spot, 1.0, 0.0).astype(BF16)

        def scatter(k, carry):
            terms = products[pl.ds(k, blocks, stride=K), :].astype(BF16)
            partial[pl.ds(k, devices, stride=2 * K), :] = dot(chosen, terms)
            return carry

        lax.fori_loop(0, K, scatter, 0)
        terms = [
            dot(top_blocks_ref[b * K : (b + 1) * K, :], top_coeffs[top_source_ref[b]])
            for b in range(top_blocks)
        ]
        for t in range(devices // 8):
            total = jnp.zeros((K, RHS), F32)
            for b in range(top_blocks):
                total = total + jnp.where(top_target_ref[b : b + 1, :] == t, 1.0, 0.0) * terms[b]
            for j in range(8):
                first = spot_of(t * 8 + j) * 2 * K + K
                partial[first : first + K, :] = total

    def reduced_core():
        mine = partial[rows(core, half * 2 * K), :]
        currents[-1][...] = (mine + core_got[...]).astype(BF16)

    def reduced(level):
        stride, size = levels[level]
        total = currents[level][rows(digit(stride, size), stride * 2 * K), :].astype(F32)
        for turn in range(1, size):
            total = total + receives[level][turn - 1].astype(F32)
        return total

    own_points.wait()
    featured(1)
    start(gather_copies(0))
    send_chunk(2)

    @pl.when(has_before)
    def _():
        points_up().wait_recv()

    @pl.when(has_after)
    def _():
        points_down().wait_recv()

    featured(0)
    featured(2)
    send_chunk(3)

    stages = []
    for level in range(len(levels)):
        def gather(level=level):
            arrived(gather_copies(level))
            start(gather_copies(level + 1))
        stages.append((2 * level + 1, gather))
    at = 2 * len(levels) + 1

    def coupled():
        arrived(gather_copies(len(levels)))
        couple()

    stages.append((at, coupled))
    stages.append((at + 1, lambda: start(reduce_copies(len(levels)))))

    def core_reduced():
        arrived(reduce_copies(len(levels)))
        reduced_core()

    stages.append((at + 3, core_reduced))
    at += 4
    for level in range(len(levels) - 1, -1, -1):
        stages.append((at, lambda level=level: start(reduce_copies(level))))
        if level:
            def reduce(level=level):
                arrived(reduce_copies(level))
                currents[level - 1][...] = reduced(level).astype(BF16)
            stages.append((at + 3, reduce))
        at += 4

    def made_copy(i, slot):
        return pltpu.make_async_copy(
            made.at[slot], kernels_ref.at[pl.ds(i * EACH, EACH)], made_sem.at[slot]
        )

    steps = leaves // EACH

    def make(i, carry):
        for when, stage in stages:
            pl.when(i == when)(stage)

        @pl.when((i % 2 == 0) & (i < 2 * (CHUNKS - 4)))
        def _():
            send_chunk(4 + i // 2)

        slot = i % 2

        @pl.when(i >= 2)
        def _():
            made_copy(i - 2, slot).wait()

        for k in range(EACH):
            leaf = i * EACH + k
            mine = targets[:, rows(leaf, M)].T.astype(BF16)
            for group in groups_of(named):
                theirs = jnp.concatenate(
                    [features[near_ref[leaf, j]] for j in group], axis=1
                )
                squares = dot(mine, theirs)
                made[slot, k, :, group[0] * M : (group[-1] + 1) * M] = lax.rsqrt(
                    squares.astype(BF16)
                )
        made_copy(i, slot).start()
        return carry

    lax.fori_loop(0, steps, make, 0)
    arrived(reduce_copies(0))
    total = reduced(0)
    base = (total[:K] + dot(base_t_ref[...], total[K:].astype(BF16))).astype(BF16)
    mid = dot(mid_t_ref[...], base).astype(BF16)
    for m in range(leaves // 8):
        area = slice(m * 8 * K, (m + 1) * 8 * K)
        fields_ref[area, :] = dot(leaf_t_ref[area, :], mid[m * K : (m + 1) * K, :]).astype(BF16)

    made_copy(steps - 2, steps % 2).wait()
    made_copy(steps - 1, (steps - 1) % 2).wait()

    def zero(out_ref, sem):
        own[0:part, :] = jnp.zeros((part, RHS), BF16)

        def each(c, carry):
            copy = pltpu.make_async_copy(own.at[pl.ds(0, part), :], out_ref.at[rows(c, part), :], sem)
            copy.start()
            copy.wait()
            return carry

        lax.fori_loop(0, CHUNKS, each, 0)

    for level in range(len(levels) + 1):
        sent(gather_copies(level))
        sent(reduce_copies(level))

    def drain_up(c, carry):
        chunk_up(c).wait_send()
        return carry

    def drain_down(c, carry):
        chunk_down(c).wait_send()
        return carry

    @pl.when(has_after)
    def _():
        points_up().wait_send()
        lax.fori_loop(0, CHUNKS, drain_up, 0)
        remote(charges_ref, after_ref, up_send.at[0], near_recv.at[1], me + 1).wait_recv()

    @pl.when(has_before)
    def _():
        points_down().wait_send()
        lax.fori_loop(0, CHUNKS, drain_down, 0)
        remote(charges_ref, before_ref, up_send.at[0], near_recv.at[0], me - 1).wait_recv()

    @pl.when(jnp.logical_not(has_before))
    def _():
        zero(before_ref, local_sem.at[0])

    @pl.when(jnp.logical_not(has_after))
    def _():
        zero(after_ref, local_sem.at[0])


def use_kernel(
    leaves, named,
    near_ref, kernel_ref, before_ref, own_ref, after_ref, fields_ref, basis_ref, out_ref,
    pool, sems,
):
    points = leaves * M

    @pl.when(pl.program_id(0) == 0)
    def _():
        copies = [
            pltpu.make_async_copy(ref, pool.at[pl.ds(i * points, points), :], sems.at[i])
            for i, ref in enumerate((before_ref, own_ref, after_ref))
        ]
        for copy in copies:
            copy.start()
        for copy in copies:
            copy.wait()

    for k in range(kernel_ref.shape[0]):
        leaf = pl.program_id(0) * kernel_ref.shape[0] + k
        total = dot_ta(basis_ref[rows(leaf, K), :], fields_ref[rows(leaf, K), :])
        for group in groups_of(named):
            theirs = jnp.concatenate([pool[rows(near_ref[leaf, j], M), :] for j in group], axis=0)
            total = total + dot(kernel_ref[k, :, group[0] * M : (group[-1] + 1) * M], theirs)
        out_ref[k * M : (k + 1) * M, :] = total.astype(BF16)


def per_device(
    coords,
    charges,
    near_leaves,
    leaf_basis,
    leaf_transfer,
    mid_transfer,
    base_transfer,
    base_coupling,
    base_target,
    base_source,
    top_coupling,
    top_target,
    top_source,
):
    leaves, named = near_leaves.shape
    devices = lax.axis_size("leaf")
    blocks, top_blocks = base_coupling.shape[0], top_coupling.shape[0]
    scale = math.sqrt(named * M)
    count = leaves * M
    half = devices // 2
    levels = levels_of(devices)
    widest = max(size for _, size in levels)
    basis = leaf_basis.reshape(-1, M)
    leaf_t = leaf_transfer.reshape(-1, K)
    mid_t = mid_transfer.reshape(-1, K)
    base_t = base_transfer.reshape(-1, K)

    step = max(s for s in range(1, 33) if blocks % s == 0)
    kernels, before, after, fields = pl.pallas_call(
        functools.partial(
            exchange_kernel, devices, leaves, named, blocks, top_blocks, step, scale
        ),
        out_shape=[
            jax.ShapeDtypeStruct((leaves, M, named * M), BF16),
            jax.ShapeDtypeStruct((count, RHS), BF16),
            jax.ShapeDtypeStruct((count, RHS), BF16),
            jax.ShapeDtypeStruct((leaves * K, RHS), BF16),
        ],
        in_specs=[SMEM] * 3 + [ANY] * 2 + [VMEM] * 8,
        out_specs=[ANY] * 3 + [VMEM],
        scratch_shapes=[
            pltpu.VMEM((3, 3, count), F32),
            pltpu.VMEM((count, RHS), BF16),
            pltpu.VMEM((3 * leaves, FEATURES, M), BF16),
            pltpu.VMEM((FEATURES, count), F32),
            pltpu.VMEM((FEATURES, WIDTH), F32),
            pltpu.VMEM((2, EACH, M, named * M), BF16),
            pltpu.VMEM((leaves * K, RHS), BF16),
            pltpu.VMEM((devices, 2 * K, RHS), BF16),
            pltpu.VMEM((blocks * K, RHS), F32),
            pltpu.VMEM((devices * 2 * K, RHS), F32),
            pltpu.VMEM((half * 2 * K, RHS), F32),
            pltpu.VMEM((devices // 8, K, RHS), BF16),
        ]
        + [pltpu.VMEM((stride * size * 2 * K, RHS), BF16) for stride, size in levels]
        + [pltpu.VMEM((size - 1, stride * 2 * K, RHS), BF16) for stride, size in levels]
        + [
            pltpu.SemaphoreType.DMA((2,)),
            pltpu.SemaphoreType.DMA((2,)),
            pltpu.SemaphoreType.DMA((2,)),
            pltpu.SemaphoreType.DMA((2,)),
            pltpu.SemaphoreType.DMA((CHUNKS,)),
            pltpu.SemaphoreType.DMA((CHUNKS,)),
            pltpu.SemaphoreType.DMA((2,)),
        ]
        + [pltpu.SemaphoreType.DMA((len(levels) + 1, widest - 1))] * 4,
        compiler_params=pltpu.CompilerParams(
            vmem_limit_bytes=60 * 1024 * 1024, collective_id=0, has_side_effects=True
        ),
        cost_estimate=pl.CostEstimate(
            flops=16_000_000_000, bytes_accessed=70_000_000, transcendentals=28_000_000
        ),
        name="exchange",
    )(
        near_leaves, base_source, top_source, coords, charges,
        top_target.reshape(-1, 1), base_target.reshape(1, blocks), basis, leaf_t, mid_t, base_t,
        base_coupling.reshape(-1, K), top_coupling.reshape(-1, K),
    )
    each = 4
    return pl.pallas_call(
        functools.partial(use_kernel, leaves, named),
        grid=(leaves // each,),
        out_shape=jax.ShapeDtypeStruct((count, RHS), BF16),
        in_specs=[SMEM, pl.BlockSpec((each, M, named * M), lambda i: (i, 0, 0)), ANY, ANY, ANY]
        + [VMEM] * 2,
        out_specs=pl.BlockSpec((each * M, RHS), lambda i: (i, 0)),
        scratch_shapes=[
            pltpu.VMEM((3 * count, RHS), BF16),
            pltpu.SemaphoreType.DMA((3,)),
        ],
        compiler_params=pltpu.CompilerParams(vmem_limit_bytes=48 * 1024 * 1024),
        cost_estimate=pl.CostEstimate(
            flops=8_000_000_000, bytes_accessed=66_000_000, transcendentals=0
        ),
        name="use",
    )(near_leaves, kernels, before, charges, after, fields, basis)


def solution(mesh):
    split, flat = P("leaf", None), P("leaf")
    in_specs = (P(None, "leaf"),) + (split,) * 8 + (flat, split, flat, flat)
    return jax.shard_map(
        per_device, mesh=mesh, in_specs=in_specs, out_specs=split, check_vma=False
    )
```

time: 148 us -> 132 us (0.89)
  Pallas kernels: 65.5 us -> 115 us
  blocking collectives: 46.7 us -> 0 us
  starting transfers between devices: 12 us -> 0 us
  waiting for transfers between devices: 11.9 us -> 0 us
  local copies, waits for them, and re-layouts: 9.88 us -> 15.5 us
    pallas_call x4 -> x2, Pallas kernels: 65.5 us -> 115 us  [the longest x1 84.6 us: per_device(): pl.pallas_call(functools.partial(exchange_kernel, devices, leaves, named,...]
    all_gather x1 -> x0, blocking collectives: 46.7 us -> none  [per_device(): gathered = lax.all_gather(mine, 'leaf', axis=0, tiled=True)]
    all_to_all x1 -> x0, waiting for transfers between devices: 11.8 us -> none  [per_device(): lax.all_to_all(partial, 'leaf', split_axis=0, concat_axis=0, tiled=True)]
    ppermute x4 -> x0, starting transfers between devices: 9.35 us -> none  [the longest x1 4.38 us: per_device(): charges_before = lax.ppermute(outgoing, 'leaf', up)]
    all_to_all x1 -> x0, starting transfers between devices: 2.61 us -> none  [per_device(): lax.all_to_all(partial, 'leaf', split_axis=0, concat_axis=0, tiled=True)]
    unnamed x25 -> x13, local copies, waits for them, and re-layouts: 4.04 us -> 4.05 us
  transfers between devices with their start and end apart: 5 -> 0, of which waited for: 1 -> 0; matrix products, arithmetic and copies ran while one was open for 5% -> 0% of each run, Pallas kernels for 23% -> 0%
where the time goes in v1:
time: 132 us
  Pallas kernels  115 us (87%)
  local copies, waits for them, and re-layouts  15.5 us (12%)
    pallas_call x1, Pallas kernels, per_device(): pl.pallas_call(functools.partial(exchange_kernel, devices, leaves, named,...  84.6 us
    pallas_call x1, Pallas kernels, per_device(): pl.pallas_call(functools.partial(use_kernel, leaves, named), grid=(leaves...  30.6 us
    unnamed x13, local copies, waits for them, and re-layouts  4.05 us

profile of v1, /device:TPU:0, one launch (start us, length us, event | category | flops | bytes accessed | tf_op | source)
XLA Modules:
  0.0 131.5 jit_solution(15392258909014982286)
XLA Ops:
  0.0 0.0 copy-start.5
  0.0 0.8 reduce
  0.8 1.3 %copy.18.top_target_ref = s32[8,1]{1,0:T(8,128)} copy(s32[8,1]{0,1:T(1,128)} %bitcast.2) | data formatting | bytes 64 | tf_op jit(solution)/shard_map/reshape | solution.py:561
  2.1 0.7 reshape.29.base_t_ref
  2.7 1.4 %copy.19.near_ref = s32[64,27]{1,0:T(8,128)} copy(s32[64,27]{0,1:T(8,128)} %param.15) | data formatting | bytes 13824 | tf_op args[2]
  4.2 1.5 %reshape.28.mid_t_ref = bf16[256,32]{1,0:T(8,128)(2,1)} reshape(bf16[8,1024]{1,0:T(8,128)(2,1)} %param.18) | data formatting | bytes 32768 | tf_op jit(solution)/shard_map/reshape | solution.py:510
  5.6 1.5 %reshape.31.top_blocks_ref = bf16[256,32]{1,0:T(8,128)(2,1)} reshape(bf16[8,1024]{1,0:T(8,128)(2,1)} %param.23) | data formatting | bytes 32768 | tf_op jit(solution)/shard_map/reshape | solution.py:562
  7.1 2.1 %reshape.26.basis_ref = bf16[2048,128]{1,0:T(8,128)(2,1)} reshape(bf16[64,4096]{1,0:T(8,128)(2,1)} %param.16) | data formatting | bytes 1048576 | tf_op jit(solution)/shard_map/reshape | solution.py:508
  9.2 2.1 %reshape.27.leaf_t_ref = bf16[2048,32]{1,0:T(8,128)(2,1)} reshape(bf16[64,1024]{1,0:T(8,128)(2,1)} %param.17) | data formatting | bytes 262144 | tf_op jit(solution)/shard_map/reshape | solution.py:509
  11.3 0.0 copy-done.5
  11.3 2.3 %reshape.30.blocks_ref = bf16[6048,32]{1,0:T(8,128)(2,1)} reshape(bf16[189,1024]{1,0:T(8,128)(2,1)S(1)} %copy-done.5) | data formatting | bytes 774144 | tf_op jit(solution)/shard_map/reshape | solution.py:562
  13.6 0.0 copy-start
  13.6 0.0 copy-start.1
  13.6 0.0 copy-start.4
  13.6 84.6 %exchange.1 = (bf16[64,128,3456]{2,1,0:T(8,128)(2,1)}, bf16[8192,128]{1,0:T(8,128)(2,1)}, bf16[8192,128]{1,0:T(8,128)(2,1)}, bf16[2048,128]{1,0:T(8,128)(2,1)}) custom-call(s32[64,27]{1,0:T(8,128)} %copy.19.near_ref, s32[189]{0:T(256)} %source_ref.1, s32[8]{0:T(128)} %top_source_ref.1, f32[3,8192]{1,0:T(4,128)} %coords_ref.1, bf16[8192,128]{1,0:T(8,128)(2,1)} %own_ref.1, ...), custom_call_target="tpu_custom_call" | custom-call | flops 16000000000 | bytes 70000000 | tf_op jit(solution)/shard_map/exchange/pallas_call | solution.py:514
  98.2 0.0 copy-done
  98.3 0.0 copy-done.1
  98.3 0.0 copy-done.4
  98.3 0.0 copy-start.2
  98.3 1.6 %copy-done.2 = bf16[8192,128]{1,0:T(8,128)(2,1)S(1)} copy-done((bf16[8192,128]{1,0:T(8,128)(2,1)S(1)}, bf16[8192,128]{1,0:T(8,128)(2,1)}, u32[]{:S(2)}) %copy-start.2) | copy-done | bytes 2097176
  99.9 0.0 copy-start.3
  99.9 1.0 copy-done.3
  100.9 30.6 %use.1 = bf16[8192,128]{1,0:T(8,128)(2,1)} custom-call(s32[64,27]{1,0:T(8,128)S(1)} %copy-done.4, bf16[64,128,3456]{2,1,0:T(8,128)(2,1)} %get-tuple-element.9.kernel_ref, bf16[8192,128]{1,0:T(8,128)(2,1)S(1)} %copy-done.2, bf16[8192,128]{1,0:T(8,128)(2,1)S(1)} %copy-done.1, bf16[8192,128]{1,0:T(8,128)(2,1)} %get-tuple-element.11.after_ref, ...), custom_call_target="tpu_custom_call" | custom-call | flops 8000000000 | bytes 66000000 | tf_op jit(solution)/shard_map/use/pallas_call | solution.py:565
Async XLA Ops:
  0.0 11.3 %copy-start.5 = (bf16[189,1024]{1,0:T(8,128)(2,1)S(1)}, bf16[189,1024]{1,0:T(8,128)(2,1)}, u32[]{:S(2)}) copy-start(bf16[189,1024]{1,0:T(8,128)(2,1)} %param.20) | copy-start | bytes 1161220
  13.6 84.6 %copy-start = (bf16[2048,128]{1,0:T(8,128)(2,1)S(1)}, bf16[2048,128]{1,0:T(8,128)(2,1)}, u32[]{:S(2)}) copy-start(bf16[2048,128]{1,0:T(8,128)(2,1)} %reshape.26.basis_ref) | copy-start | bytes 1572868
  13.6 84.7 %copy-start.1 = (bf16[8192,128]{1,0:T(8,128)(2,1)S(1)}, bf16[8192,128]{1,0:T(8,128)(2,1)}, u32[]{:S(2)}) copy-start(bf16[8192,128]{1,0:T(8,128)(2,1)} %own_ref.1) | copy-start | bytes 6291460
  13.6 84.7 %copy-start.4 = (s32[64,27]{1,0:T(8,128)S(1)}, s32[64,27]{1,0:T(8,128)}, u32[]{:S(2)}) copy-start(s32[64,27]{1,0:T(8,128)} %copy.19.near_ref) | copy-start | bytes 20740
  98.3 1.6 %copy-start.2 = (bf16[8192,128]{1,0:T(8,128)(2,1)S(1)}, bf16[8192,128]{1,0:T(8,128)(2,1)}, u32[]{:S(2)}) copy-start(bf16[8192,128]{1,0:T(8,128)(2,1)} %get-tuple-element.10.before_ref) | copy-start | bytes 6291460
  99.9 1.0 copy-start.3

commit v2 on v1

--- a/solution.py
+++ b/solution.py
@@ -15,7 +15,9 @@
 DELTA_SQ = 0.0025
 CHUNKS = 16
 EACH = 2
-WIDTH = 1024
+WIDTH = 2048
+LANES = 128
+FOLD = LANES // K
 
 F32 = jnp.float32
 BF16 = jnp.bfloat16
@@ -35,6 +37,28 @@
 
 def rows(index, size):
     return pl.ds(pl.multiple_of(index * size, size), size)
+
+
+def halves(x):
+    high = x.astype(BF16).astype(F32)
+    return high, (x - high).astype(BF16).astype(F32)
+
+
+def spread(dst, src, count):
+    lane = lax.broadcasted_iota(jnp.int32, (1, LANES), 1) // K
+    masks = [jnp.where(lane == f, 1.0, 0.0) for f in range(FOLD)]
+    for tile in range(K // FOLD):
+        slab = src[:, tile * LANES : (tile + 1) * LANES].astype(F32)
+        for f in range(FOLD):
+            dst[pl.ds(tile * FOLD + f, count, stride=K), :] = slab * masks[f]
+
+
+def folded(x):
+    return sum(x[f * K : (f + 1) * K, :] for f in range(1, FOLD)) + x[:K, :]
+
+
+def tiled(x):
+    return jnp.concatenate([x] * FOLD, axis=0)
 
 
 def pieces(x):
@@ -67,12 +91,13 @@
 
 def exchange_kernel(
     devices, leaves, named, blocks, top_blocks, step, scale,
-    near_ref, source_ref, top_source_ref,
-    coords_ref, charges_ref,
-    top_target_ref, target_ref, basis_ref, leaf_t_ref, mid_t_ref, base_t_ref, blocks_ref, top_blocks_ref,
-    kernels_ref, before_ref, after_ref, fields_ref,
-    points, own, features, targets, staged, made, coeffs, gathered,
-    products, partial, core_got, top_coeffs, *rest,
+    source_ref, top_target_ref, top_source_ref,
+    near_ref, coords_ref, charges_ref,
+    target_ref, basis_ref, leaf_t_ref, mid_t_ref, base_t_ref, blocks_ref, top_blocks_ref,
+    kernels_ref, before_ref, after_ref, fields_ref, basis_out,
+    named_leaves, points, own, features, targets, staged, made, coeffs, gathered,
+    zeros_part, basis, leaf_t, mid_t, base_t, top_t, wide, products, partial, core_got,
+    top_coeffs, *rest,
 ):
     levels = levels_of(devices)
     currents, receives = rest[: len(levels)], rest[len(levels) : 2 * len(levels)]
@@ -88,8 +113,11 @@
 
     own_copy = pltpu.make_async_copy(charges_ref, own, local_sem.at[0])
     own_points = pltpu.make_async_copy(coords_ref, points.at[1], local_sem.at[1])
+    near_copy = pltpu.make_async_copy(near_ref, named_leaves, local_sem.at[2])
     own_points.start()
     own_copy.start()
+    near_copy.start()
+    zeros_part[...] = jnp.zeros_like(zeros_part)
 
     def digit(stride, size):
         return (place // stride) % size
@@ -173,13 +201,38 @@
     send_chunk(0)
     send_chunk(1)
 
+    def fill(out_ref, sem):
+        def each(c, carry):
+            pltpu.make_async_copy(zeros_part, out_ref.at[rows(c, part), :], sem).start()
+            return carry
+
+        lax.fori_loop(0, CHUNKS, each, 0)
+
+    def filled(out_ref, sem):
+        pltpu.make_async_copy(own, out_ref, sem).wait()
+
+    @pl.when(jnp.logical_not(has_before))
+    def _():
+        fill(before_ref, local_sem.at[3])
+
+    @pl.when(jnp.logical_not(has_after))
+    def _():
+        fill(after_ref, local_sem.at[4])
+
+    for p in range(K):
+        basis[pl.ds(p, leaves, stride=K), :] = basis_ref[:, p * M : (p + 1) * M].astype(F32)
+    basis_out[...] = basis[...].astype(BF16)
+    spread(leaf_t, leaf_t_ref, leaves)
+    spread(mid_t, mid_t_ref, leaves // 8)
+    spread(base_t, base_t_ref, 1)
+
     own_copy.wait()
 
     def up_group(i, carry):
         for j in range(8):
             leaf = i * 8 + j
             coeffs[rows(leaf, K), :] = dot(
-                basis_ref[rows(leaf, K), :], own[rows(leaf, M), :]
+                basis_out[rows(leaf, K), :], own[rows(leaf, M), :]
             ).astype(BF16)
         return carry
 
@@ -187,27 +240,28 @@
     mids = []
     for m in range(leaves // 8):
         area = slice(m * 8 * K, (m + 1) * 8 * K)
-        mids.append(dot_ta(leaf_t_ref[area, :], coeffs[area, :]).astype(BF16))
-    base = dot_ta(mid_t_ref[...], jnp.concatenate(mids, axis=0)).astype(BF16)
+        mids.append(folded(dot_ta(leaf_t[area, :].astype(BF16), coeffs[area, :])).astype(BF16))
+    base = folded(dot_ta(mid_t[...].astype(BF16), jnp.concatenate(mids, axis=0))).astype(BF16)
     spot = core * half + place
     gathered[spot] = jnp.concatenate(
-        [base, dot_ta(base_t_ref[...], base).astype(BF16)], axis=0
+        [base, folded(dot_ta(base_t[...].astype(BF16), base)).astype(BF16)], axis=0
     )
 
     def featured(which):
         def chunk(i, carry):
             first = pl.multiple_of(i * WIDTH, WIDTH)
             x = (points[which, :, pl.ds(first, WIDTH)] - 0.5) * scale
-            h, m, l = pieces(x)
+            h, m = halves(x)
+            x = h + m
             norm = x[0:1] * x[0:1] + x[1:2] * x[1:2] + x[2:3] * x[2:3]
             ones = jnp.ones((3, WIDTH), F32)
-            zeros = jnp.zeros((FEATURES - 24, WIDTH), F32)
+            zeros = jnp.zeros((FEATURES - 18, WIDTH), F32)
             if which == 1:
                 n = pieces(norm + DELTA_SQ * scale * scale)
-                write_features(targets, first, WIDTH, [h, h, m, h, l, m, *n, ones, zeros])
+                write_features(targets, first, WIDTH, [h, h, m, m, *n, ones, zeros])
             n = pieces(norm)
-            h, m, l = -2.0 * h, -2.0 * m, -2.0 * l
-            write_features(staged, 0, WIDTH, [h, m, h, l, h, m, ones, *n, zeros])
+            h, m = -2.0 * h, -2.0 * m
+            write_features(staged, 0, WIDTH, [h, m, h, m, ones, *n, zeros])
             for k in range(WIDTH // M):
                 features[which * leaves + i * (WIDTH // M) + k] = staged[
                     :, k * M : (k + 1) * M
@@ -272,13 +326,16 @@
                 total = total + gathered[spot_of(t * 8 + j), K:, :].astype(F32)
             top_coeffs[t] = total.astype(BF16)
 
+        for d in range(devices):
+            wide[d] = tiled(gathered[d, :K, :])
+
         def group(i, carry):
             for j in range(step):
                 b = i * step + j
                 source = source_ref[b]
                 where = (source & 1) * half + (source >> 1)
                 products[rows(b, K), :] = dot(
-                    blocks_ref[rows(b, K), :], gathered[where, :K, :]
+                    products[rows(b, K), :].astype(BF16), wide[where]
                 )
             return carry
 
@@ -288,20 +345,22 @@
         ids = lax.broadcasted_iota(jnp.int32, (devices, blocks), 0)
         chosen = jnp.where(ids == named_spot, 1.0, 0.0).astype(BF16)
 
-        def scatter(k, carry):
-            terms = products[pl.ds(k, blocks, stride=K), :].astype(BF16)
-            partial[pl.ds(k, devices, stride=2 * K), :] = dot(chosen, terms)
+        def scatter(i, carry):
+            for j in range(8):
+                k = i * 8 + j
+                terms = products[pl.ds(k, blocks, stride=K), :].astype(BF16)
+                partial[pl.ds(k, devices, stride=2 * K), :] = dot(chosen, terms)
             return carry
 
-        lax.fori_loop(0, K, scatter, 0)
+        lax.fori_loop(0, K // 8, scatter, 0)
         terms = [
-            dot(top_blocks_ref[b * K : (b + 1) * K, :], top_coeffs[top_source_ref[b]])
+            dot(top_t[b * K : (b + 1) * K, :].astype(BF16), tiled(top_coeffs[top_source_ref[b]]))
             for b in range(top_blocks)
         ]
         for t in range(devices // 8):
             total = jnp.zeros((K, RHS), F32)
             for b in range(top_blocks):
-                total = total + jnp.where(top_target_ref[b : b + 1, :] == t, 1.0, 0.0) * terms[b]
+                total = total + jnp.where(top_target_ref[b] == t, 1.0, 0.0) * terms[b]
             for j in range(8):
                 first = spot_of(t * 8 + j) * 2 * K + K
                 partial[first : first + K, :] = total
@@ -318,8 +377,11 @@
         return total
 
     own_points.wait()
+    near_copy.wait()
     featured(1)
     start(gather_copies(0))
+    spread(products, blocks_ref, blocks)
+    spread(top_t, top_blocks_ref, top_blocks)
     send_chunk(2)
 
     @pl.when(has_before)
@@ -339,8 +401,8 @@
         def gather(level=level):
             arrived(gather_copies(level))
             start(gather_copies(level + 1))
-        stages.append((2 * level + 1, gather))
-    at = 2 * len(levels) + 1
+        stages.append((3 * level, gather))
+    at = 3 * len(levels)
 
     def coupled():
         arrived(gather_copies(len(levels)))
@@ -353,8 +415,8 @@
         arrived(reduce_copies(len(levels)))
         reduced_core()
 
-    stages.append((at + 3, core_reduced))
-    at += 4
+    stages.append((at + 4, core_reduced))
+    at += 5
     for level in range(len(levels) - 1, -1, -1):
         stages.append((at, lambda level=level: start(reduce_copies(level))))
         if level:
@@ -390,7 +452,7 @@
             mine = targets[:, rows(leaf, M)].T.astype(BF16)
             for group in groups_of(named):
                 theirs = jnp.concatenate(
-                    [features[near_ref[leaf, j]] for j in group], axis=1
+                    [features[named_leaves[j, leaf]] for j in group], axis=1
                 )
                 squares = dot(mine, theirs)
                 made[slot, k, :, group[0] * M : (group[-1] + 1) * M] = lax.rsqrt(
@@ -402,25 +464,18 @@
     lax.fori_loop(0, steps, make, 0)
     arrived(reduce_copies(0))
     total = reduced(0)
-    base = (total[:K] + dot(base_t_ref[...], total[K:].astype(BF16))).astype(BF16)
-    mid = dot(mid_t_ref[...], base).astype(BF16)
+    base = (
+        total[:K] + dot(base_t[...].astype(BF16), tiled(total[K:].astype(BF16)))
+    ).astype(BF16)
+    mid = dot(mid_t[...].astype(BF16), tiled(base)).astype(BF16)
     for m in range(leaves // 8):
         area = slice(m * 8 * K, (m + 1) * 8 * K)
-        fields_ref[area, :] = dot(leaf_t_ref[area, :], mid[m * K : (m + 1) * K, :]).astype(BF16)
+        fields_ref[area, :] = dot(
+            leaf_t[area, :].astype(BF16), tiled(mid[m * K : (m + 1) * K, :])
+        ).astype(BF16)
 
     made_copy(steps - 2, steps % 2).wait()
     made_copy(steps - 1, (steps - 1) % 2).wait()
-
-    def zero(out_ref, sem):
-        own[0:part, :] = jnp.zeros((part, RHS), BF16)
-
-        def each(c, carry):
-            copy = pltpu.make_async_copy(own.at[pl.ds(0, part), :], out_ref.at[rows(c, part), :], sem)
-            copy.start()
-            copy.wait()
-            return carry
-
-        lax.fori_loop(0, CHUNKS, each, 0)
 
     for level in range(len(levels) + 1):
         sent(gather_copies(level))
@@ -448,11 +503,11 @@
 
     @pl.when(jnp.logical_not(has_before))
     def _():
-        zero(before_ref, local_sem.at[0])
+        filled(before_ref, local_sem.at[3])
 
     @pl.when(jnp.logical_not(has_after))
     def _():
-        zero(after_ref, local_sem.at[0])
+        filled(after_ref, local_sem.at[4])
 
 
 def use_kernel(
@@ -477,7 +532,7 @@
         leaf = pl.program_id(0) * kernel_ref.shape[0] + k
         total = dot_ta(basis_ref[rows(leaf, K), :], fields_ref[rows(leaf, K), :])
         for group in groups_of(named):
-            theirs = jnp.concatenate([pool[rows(near_ref[leaf, j], M), :] for j in group], axis=0)
+            theirs = jnp.concatenate([pool[rows(near_ref[j, leaf], M), :] for j in group], axis=0)
             total = total + dot(kernel_ref[k, :, group[0] * M : (group[-1] + 1) * M], theirs)
         out_ref[k * M : (k + 1) * M, :] = total.astype(BF16)
 
@@ -505,13 +560,8 @@
     half = devices // 2
     levels = levels_of(devices)
     widest = max(size for _, size in levels)
-    basis = leaf_basis.reshape(-1, M)
-    leaf_t = leaf_transfer.reshape(-1, K)
-    mid_t = mid_transfer.reshape(-1, K)
-    base_t = base_transfer.reshape(-1, K)
-
     step = max(s for s in range(1, 33) if blocks % s == 0)
-    kernels, before, after, fields = pl.pallas_call(
+    kernels, before, after, fields, basis = pl.pallas_call(
         functools.partial(
             exchange_kernel, devices, leaves, named, blocks, top_blocks, step, scale
         ),
@@ -520,10 +570,12 @@
             jax.ShapeDtypeStruct((count, RHS), BF16),
             jax.ShapeDtypeStruct((count, RHS), BF16),
             jax.ShapeDtypeStruct((leaves * K, RHS), BF16),
+            jax.ShapeDtypeStruct((leaves * K, M), BF16),
         ],
-        in_specs=[SMEM] * 3 + [ANY] * 2 + [VMEM] * 8,
-        out_specs=[ANY] * 3 + [VMEM],
+        in_specs=[SMEM] * 3 + [ANY] * 3 + [VMEM] * 7,
+        out_specs=[ANY] * 3 + [VMEM] * 2,
         scratch_shapes=[
+            pltpu.SMEM((named, leaves), jnp.int32),
             pltpu.VMEM((3, 3, count), F32),
             pltpu.VMEM((count, RHS), BF16),
             pltpu.VMEM((3 * leaves, FEATURES, M), BF16),
@@ -532,6 +584,13 @@
             pltpu.VMEM((2, EACH, M, named * M), BF16),
             pltpu.VMEM((leaves * K, RHS), BF16),
             pltpu.VMEM((devices, 2 * K, RHS), BF16),
+            pltpu.VMEM((count // CHUNKS, RHS), BF16),
+            pltpu.VMEM((leaves * K, M), F32),
+            pltpu.VMEM((leaves * K, LANES), F32),
+            pltpu.VMEM((leaves // 8 * K, LANES), F32),
+            pltpu.VMEM((K, LANES), F32),
+            pltpu.VMEM((top_blocks * K, LANES), F32),
+            pltpu.VMEM((devices, LANES, RHS), BF16),
             pltpu.VMEM((blocks * K, RHS), F32),
             pltpu.VMEM((devices * 2 * K, RHS), F32),
             pltpu.VMEM((half * 2 * K, RHS), F32),
@@ -540,7 +599,7 @@
         + [pltpu.VMEM((stride * size * 2 * K, RHS), BF16) for stride, size in levels]
         + [pltpu.VMEM((size - 1, stride * 2 * K, RHS), BF16) for stride, size in levels]
         + [
-            pltpu.SemaphoreType.DMA((2,)),
+            pltpu.SemaphoreType.DMA((5,)),
             pltpu.SemaphoreType.DMA((2,)),
             pltpu.SemaphoreType.DMA((2,)),
             pltpu.SemaphoreType.DMA((2,)),
@@ -557,9 +616,9 @@
         ),
         name="exchange",
     )(
-        near_leaves, base_source, top_source, coords, charges,
-        top_target.reshape(-1, 1), base_target.reshape(1, blocks), basis, leaf_t, mid_t, base_t,
-        base_coupling.reshape(-1, K), top_coupling.reshape(-1, K),
+        base_source, top_target, top_source, near_leaves.T, coords, charges,
+        base_target.T, leaf_basis, leaf_transfer, mid_transfer, base_transfer,
+        base_coupling, top_coupling,
     )
     each = 4
     return pl.pallas_call(
@@ -573,12 +632,12 @@
             pltpu.VMEM((3 * count, RHS), BF16),
             pltpu.SemaphoreType.DMA((3,)),
         ],
-        compiler_params=pltpu.CompilerParams(vmem_limit_bytes=48 * 1024 * 1024),
+        compiler_params=pltpu.CompilerParams(vmem_limit_bytes=60 * 1024 * 1024),
         cost_estimate=pl.CostEstimate(
             flops=8_000_000_000, bytes_accessed=66_000_000, transcendentals=0
         ),
         name="use",
-    )(near_leaves, kernels, before, charges, after, fields, basis)
+    )(near_leaves.T, kernels, before, charges, after, fields, basis)
 
 
 def solution(mesh):

time: 132 us -> 101 us (0.77)
  local copies, waits for them, and re-layouts: 15.5 us -> 0 us
  Pallas kernels: 115 us -> 100 us
    pallas_call x1, Pallas kernels: 84.6 us -> 68.3 us  [per_device(): pl.pallas_call(functools.partial(exchange_kernel, devices, leaves, named,...]
    reshape x7 -> x0, local copies, waits for them, and re-layouts: 11.4 us -> none  [the longest x1 2.34 us: per_device(): base_coupling.reshape(-1, K)]
    unnamed x13 -> x0, local copies, waits for them, and re-layouts: 4.05 us -> none
    pallas_call x1, Pallas kernels: 30.6 us -> 32.1 us  [per_device(): pl.pallas_call(functools.partial(use_kernel, leaves, named), grid=(leaves...]
where the time goes in v2:
time: 101 us; the launch traced here: 100 us
  Pallas kernels  100 us (99%)
    pallas_call x1, Pallas kernels, per_device(): pl.pallas_call(functools.partial(exchange_kernel, devices, leaves, named,...  68.3 us
    pallas_call x1, Pallas kernels, per_device(): pl.pallas_call(functools.partial(use_kernel, leaves, named), grid=(leaves...  32.1 us

profile of v2, /device:TPU:0, one launch (start us, length us, event | category | flops | bytes accessed | tf_op | source)
XLA Modules:
  0.0 100.3 jit_solution(10215677433910288663)
XLA Ops:
  0.0 68.3 %exchange.1 = (bf16[64,128,3456]{2,1,0:T(8,128)(2,1)}, bf16[8192,128]{1,0:T(8,128)(2,1)}, bf16[8192,128]{1,0:T(8,128)(2,1)}, bf16[2048,128]{1,0:T(8,128)(2,1)}, bf16[2048,128]{1,0:T(8,128)(2,1)}) custom-call(s32[189]{0:T(256)} %source_ref.1, s32[8]{0:T(128)} %top_target_ref.1, s32[8]{0:T(128)} %top_source_ref.1, s32[27,64]{1,0:T(8,128)} %bitcast.2, ...), custom_call_target="tpu_custom_call" | custom-call | flops 16000000000 | bytes 70000000 | tf_op jit(solution)/shard_map/exchange/pallas_call | solution.py:564
  68.3 32.1 %use.1 = bf16[8192,128]{1,0:T(8,128)(2,1)} custom-call(s32[27,64]{1,0:T(8,128)} %bitcast.3, bf16[64,128,3456]{2,1,0:T(8,128)(2,1)} %get-tuple-element.10.kernel_ref, bf16[8192,128]{1,0:T(8,128)(2,1)} %get-tuple-element.11.before_ref, bf16[8192,128]{1,0:T(8,128)(2,1)} %own_ref.1, bf16[8192,128]{1,0:T(8,128)(2,1)} %get-tuple-element.12.after_ref, ...), custom_call_target="tpu_custom_call" | custom-call | flops 8000000000 | bytes 66000000 | tf_op jit(solution)/shard_map/use/pallas_call | solution.py:624

commit v3 on v2

--- a/solution.py
+++ b/solution.py
@@ -14,7 +14,8 @@
 FEATURES = 32
 DELTA_SQ = 0.0025
 CHUNKS = 16
-EACH = 2
+EACH = 4
+KEEP = 36
 WIDTH = 2048
 LANES = 128
 FOLD = LANES // K
@@ -94,30 +95,29 @@
     source_ref, top_target_ref, top_source_ref,
     near_ref, coords_ref, charges_ref,
     target_ref, basis_ref, leaf_t_ref, mid_t_ref, base_t_ref, blocks_ref, top_blocks_ref,
-    kernels_ref, before_ref, after_ref, fields_ref, basis_out,
-    named_leaves, points, own, features, targets, staged, made, coeffs, gathered,
-    zeros_part, basis, leaf_t, mid_t, base_t, top_t, wide, products, partial, core_got,
+    out_ref, spill_ref,
+    named_leaves, points, pool, slots, outs, fields, basis_out, features, targets, staged, coeffs, gathered,
+    basis, leaf_t, mid_t, base_t, top_t, wide, products, partial, core_got,
     top_coeffs, *rest,
 ):
     levels = levels_of(devices)
     currents, receives = rest[: len(levels)], rest[len(levels) : 2 * len(levels)]
-    (local_sem, made_sem, point_send, point_recv, up_send, down_send, near_recv,
+    (local_sem, spill_sem, fill_sem, out_sem, point_send, point_recv, up_send, down_send, near_recv,
      gather_send, gather_recv, reduce_send, reduce_recv) = rest[2 * len(levels) :]
     count = leaves * M
-    part = count // CHUNKS
+    part = leaves // CHUNKS
     half = devices // 2
     me = lax.axis_index("leaf")
     core, place = me % 2, me // 2
     has_before, has_after = me > 0, me < devices - 1
     twin = place * 2 + (1 - core)
 
-    own_copy = pltpu.make_async_copy(charges_ref, own, local_sem.at[0])
+    own_copy = pltpu.make_async_copy(charges_ref, pool.at[pl.ds(leaves, leaves)], local_sem.at[0])
     own_points = pltpu.make_async_copy(coords_ref, points.at[1], local_sem.at[1])
     near_copy = pltpu.make_async_copy(near_ref, named_leaves, local_sem.at[2])
     own_points.start()
     own_copy.start()
     near_copy.start()
-    zeros_part[...] = jnp.zeros_like(zeros_part)
 
     def digit(stride, size):
         return (place // stride) % size
@@ -163,13 +163,13 @@
 
     def chunk_up(c):
         return remote(
-            charges_ref.at[rows(c, part), :], before_ref.at[rows(c, part), :],
+            charges_ref.at[rows(c, part)], pool.at[rows(c, part)],
             up_send.at[c], near_recv.at[0], me + 1,
         )
 
     def chunk_down(c):
         return remote(
-            charges_ref.at[rows(c, part), :], after_ref.at[rows(c, part), :],
+            charges_ref.at[rows(c, part)], pool.at[rows(2 * CHUNKS + c, part)],
             down_send.at[c], near_recv.at[1], me - 1,
         )
 
@@ -193,31 +193,15 @@
     @pl.when(jnp.logical_not(has_before))
     def _():
         points[0] = jnp.zeros((3, count), F32)
+        pool[:leaves] = jnp.zeros((leaves, M, RHS), BF16)
 
     @pl.when(jnp.logical_not(has_after))
     def _():
         points[2] = jnp.zeros((3, count), F32)
+        pool[2 * leaves :] = jnp.zeros((leaves, M, RHS), BF16)
 
     send_chunk(0)
     send_chunk(1)
-
-    def fill(out_ref, sem):
-        def each(c, carry):
-            pltpu.make_async_copy(zeros_part, out_ref.at[rows(c, part), :], sem).start()
-            return carry
-
-        lax.fori_loop(0, CHUNKS, each, 0)
-
-    def filled(out_ref, sem):
-        pltpu.make_async_copy(own, out_ref, sem).wait()
-
-    @pl.when(jnp.logical_not(has_before))
-    def _():
-        fill(before_ref, local_sem.at[3])
-
-    @pl.when(jnp.logical_not(has_after))
-    def _():
-        fill(after_ref, local_sem.at[4])
 
     for p in range(K):
         basis[pl.ds(p, leaves, stride=K), :] = basis_ref[:, p * M : (p + 1) * M].astype(F32)
@@ -232,7 +216,7 @@
         for j in range(8):
             leaf = i * 8 + j
             coeffs[rows(leaf, K), :] = dot(
-                basis_out[rows(leaf, K), :], own[rows(leaf, M), :]
+                basis_out[rows(leaf, K), :], pool[leaves + leaf]
             ).astype(BF16)
         return carry
 
@@ -401,64 +385,71 @@
         def gather(level=level):
             arrived(gather_copies(level))
             start(gather_copies(level + 1))
-        stages.append((3 * level, gather))
-    at = 3 * len(levels)
+        stages.append((level, gather))
 
     def coupled():
         arrived(gather_copies(len(levels)))
         couple()
 
-    stages.append((at, coupled))
-    stages.append((at + 1, lambda: start(reduce_copies(len(levels)))))
-
     def core_reduced():
         arrived(reduce_copies(len(levels)))
         reduced_core()
 
-    stages.append((at + 4, core_reduced))
-    at += 5
+    stages.append((3, coupled))
+    stages.append((4, lambda: start(reduce_copies(len(levels)))))
+    stages.append((5, core_reduced))
+    at = 6
     for level in range(len(levels) - 1, -1, -1):
         stages.append((at, lambda level=level: start(reduce_copies(level))))
         if level:
             def reduce(level=level):
                 arrived(reduce_copies(level))
                 currents[level - 1][...] = reduced(level).astype(BF16)
-            stages.append((at + 3, reduce))
-        at += 4
-
-    def made_copy(i, slot):
+            stages.append((at + 1, reduce))
+        at += 2
+
+    steps, kept = leaves // EACH, KEEP // EACH
+    spilled = steps - kept
+
+    def spill_copy(i):
         return pltpu.make_async_copy(
-            made.at[slot], kernels_ref.at[pl.ds(i * EACH, EACH)], made_sem.at[slot]
+            slots.at[rows(i, EACH)], spill_ref.at[rows(i, EACH)], spill_sem.at[i]
         )
 
-    steps = leaves // EACH
+    def fill_copy(i):
+        return pltpu.make_async_copy(
+            spill_ref.at[rows(i, EACH)], slots.at[rows(i, EACH)], fill_sem.at[i]
+        )
+
+    def out_copy(step, slot):
+        return pltpu.make_async_copy(
+            outs.at[slot], out_ref.at[rows(step, EACH * M), :], out_sem.at[slot]
+        )
 
     def make(i, carry):
         for when, stage in stages:
             pl.when(i == when)(stage)
 
-        @pl.when((i % 2 == 0) & (i < 2 * (CHUNKS - 4)))
-        def _():
-            send_chunk(4 + i // 2)
-
-        slot = i % 2
-
-        @pl.when(i >= 2)
-        def _():
-            made_copy(i - 2, slot).wait()
+        @pl.when((i < 8) | (i % 2 == 1))
+        def _():
+            send_chunk(4 + jnp.where(i < 8, i, 8 + (i - 9) // 2))
+
+        @pl.when(i >= kept)
+        def _():
+            spill_copy(i - kept).wait()
 
         for k in range(EACH):
             leaf = i * EACH + k
             mine = targets[:, rows(leaf, M)].T.astype(BF16)
-            for group in groups_of(named):
-                theirs = jnp.concatenate(
-                    [features[named_leaves[j, leaf]] for j in group], axis=1
-                )
-                squares = dot(mine, theirs)
-                made[slot, k, :, group[0] * M : (group[-1] + 1) * M] = lax.rsqrt(
-                    squares.astype(BF16)
-                )
-        made_copy(i, slot).start()
+            theirs = jnp.concatenate(
+                [features[named_leaves[j, leaf]] for j in range(named)], axis=1
+            )
+            slots[(i % kept) * EACH + k] = lax.rsqrt(dot(mine, theirs).astype(BF16))
+
+        @pl.when(i < spilled)
+        def _():
+            spill_copy(i).start()
+
         return carry
 
     lax.fori_loop(0, steps, make, 0)
@@ -470,12 +461,53 @@
     mid = dot(mid_t[...].astype(BF16), tiled(base)).astype(BF16)
     for m in range(leaves // 8):
         area = slice(m * 8 * K, (m + 1) * 8 * K)
-        fields_ref[area, :] = dot(
+        fields[area, :] = dot(
             leaf_t[area, :].astype(BF16), tiled(mid[m * K : (m + 1) * K, :])
         ).astype(BF16)
 
-    made_copy(steps - 2, steps % 2).wait()
-    made_copy(steps - 1, (steps - 1) % 2).wait()
+    @pl.when(has_after)
+    def _():
+        remote(
+            charges_ref, pool.at[pl.ds(2 * leaves, leaves)], up_send.at[0], near_recv.at[1], me + 1
+        ).wait_recv()
+
+    @pl.when(has_before)
+    def _():
+        remote(
+            charges_ref, pool.at[pl.ds(0, leaves)], up_send.at[0], near_recv.at[0], me - 1
+        ).wait_recv()
+
+    def use(i, carry):
+        block = jnp.where(i < spilled, i + kept, jnp.where(i < kept, i, i - kept))
+        slot = i % 2
+
+        @pl.when(i >= kept)
+        def _():
+            fill_copy(i - kept).wait()
+
+        @pl.when(i >= 2)
+        def _():
+            out_copy(i, slot).wait()
+
+        for k in range(EACH):
+            leaf = block * EACH + k
+            near = jnp.concatenate(
+                [pool[named_leaves[j, leaf]] for j in range(named)], axis=0
+            )
+            total = dot(slots[(i % kept) * EACH + k], near)
+            total = total + dot_ta(basis_out[rows(leaf, K), :], fields[rows(leaf, K), :])
+            outs[slot, k * M : (k + 1) * M, :] = total.astype(BF16)
+        out_copy(block, slot).start()
+
+        @pl.when(i < spilled)
+        def _():
+            fill_copy(i).start()
+
+        return carry
+
+    lax.fori_loop(0, steps, use, 0)
+    out_copy(0, 0).wait()
+    out_copy(1, 1).wait()
 
     for level in range(len(levels) + 1):
         sent(gather_copies(level))
@@ -493,48 +525,11 @@
     def _():
         points_up().wait_send()
         lax.fori_loop(0, CHUNKS, drain_up, 0)
-        remote(charges_ref, after_ref, up_send.at[0], near_recv.at[1], me + 1).wait_recv()
 
     @pl.when(has_before)
     def _():
         points_down().wait_send()
         lax.fori_loop(0, CHUNKS, drain_down, 0)
-        remote(charges_ref, before_ref, up_send.at[0], near_recv.at[0], me - 1).wait_recv()
-
-    @pl.when(jnp.logical_not(has_before))
-    def _():
-        filled(before_ref, local_sem.at[3])
-
-    @pl.when(jnp.logical_not(has_after))
-    def _():
-        filled(after_ref, local_sem.at[4])
-
-
-def use_kernel(
-    leaves, named,
-    near_ref, kernel_ref, before_ref, own_ref, after_ref, fields_ref, basis_ref, out_ref,
-    pool, sems,
-):
-    points = leaves * M
-
-    @pl.when(pl.program_id(0) == 0)
-    def _():
-        copies = [
-            pltpu.make_async_copy(ref, pool.at[pl.ds(i * points, points), :], sems.at[i])
-            for i, ref in enumerate((before_ref, own_ref, after_ref))
-        ]
-        for copy in copies:
-            copy.start()
-        for copy in copies:
-            copy.wait()
-
-    for k in range(kernel_ref.shape[0]):
-        leaf = pl.program_id(0) * kernel_ref.shape[0] + k
-        total = dot_ta(basis_ref[rows(leaf, K), :], fields_ref[rows(leaf, K), :])
-        for group in groups_of(named):
-            theirs = jnp.concatenate([pool[rows(near_ref[j, leaf], M), :] for j in group], axis=0)
-            total = total + dot(kernel_ref[k, :, group[0] * M : (group[-1] + 1) * M], theirs)
-        out_ref[k * M : (k + 1) * M, :] = total.astype(BF16)
 
 
 def per_device(
@@ -561,30 +556,29 @@
     levels = levels_of(devices)
     widest = max(size for _, size in levels)
     step = max(s for s in range(1, 33) if blocks % s == 0)
-    kernels, before, after, fields, basis = pl.pallas_call(
+    out, _ = pl.pallas_call(
         functools.partial(
             exchange_kernel, devices, leaves, named, blocks, top_blocks, step, scale
         ),
         out_shape=[
-            jax.ShapeDtypeStruct((leaves, M, named * M), BF16),
             jax.ShapeDtypeStruct((count, RHS), BF16),
-            jax.ShapeDtypeStruct((count, RHS), BF16),
-            jax.ShapeDtypeStruct((leaves * K, RHS), BF16),
-            jax.ShapeDtypeStruct((leaves * K, M), BF16),
+            jax.ShapeDtypeStruct((leaves - KEEP, M, named * M), BF16),
         ],
         in_specs=[SMEM] * 3 + [ANY] * 3 + [VMEM] * 7,
-        out_specs=[ANY] * 3 + [VMEM] * 2,
+        out_specs=[ANY] * 2,
         scratch_shapes=[
             pltpu.SMEM((named, leaves), jnp.int32),
             pltpu.VMEM((3, 3, count), F32),
-            pltpu.VMEM((count, RHS), BF16),
+            pltpu.VMEM((3 * leaves, M, RHS), BF16),
+            pltpu.VMEM((KEEP, M, named * M), BF16),
+            pltpu.VMEM((2, EACH * M, RHS), BF16),
+            pltpu.VMEM((leaves * K, RHS), BF16),
+            pltpu.VMEM((leaves * K, M), BF16),
             pltpu.VMEM((3 * leaves, FEATURES, M), BF16),
             pltpu.VMEM((FEATURES, count), F32),
             pltpu.VMEM((FEATURES, WIDTH), F32),
-            pltpu.VMEM((2, EACH, M, named * M), BF16),
             pltpu.VMEM((leaves * K, RHS), BF16),
             pltpu.VMEM((devices, 2 * K, RHS), BF16),
-            pltpu.VMEM((count // CHUNKS, RHS), BF16),
             pltpu.VMEM((leaves * K, M), F32),
             pltpu.VMEM((leaves * K, LANES), F32),
             pltpu.VMEM((leaves // 8 * K, LANES), F32),
@@ -599,7 +593,9 @@
         + [pltpu.VMEM((stride * size * 2 * K, RHS), BF16) for stride, size in levels]
         + [pltpu.VMEM((size - 1, stride * 2 * K, RHS), BF16) for stride, size in levels]
         + [
-            pltpu.SemaphoreType.DMA((5,)),
+            pltpu.SemaphoreType.DMA((3,)),
+            pltpu.SemaphoreType.DMA(((leaves - KEEP) // EACH,)),
+            pltpu.SemaphoreType.DMA(((leaves - KEEP) // EACH,)),
             pltpu.SemaphoreType.DMA((2,)),
             pltpu.SemaphoreType.DMA((2,)),
             pltpu.SemaphoreType.DMA((2,)),
@@ -609,35 +605,19 @@
         ]
         + [pltpu.SemaphoreType.DMA((len(levels) + 1, widest - 1))] * 4,
         compiler_params=pltpu.CompilerParams(
-            vmem_limit_bytes=60 * 1024 * 1024, collective_id=0, has_side_effects=True
+            vmem_limit_bytes=63 * 1024 * 1024, collective_id=0, has_side_effects=True
         ),
         cost_estimate=pl.CostEstimate(
             flops=16_000_000_000, bytes_accessed=70_000_000, transcendentals=28_000_000
         ),
         name="exchange",
     )(
-        base_source, top_target, top_source, near_leaves.T, coords, charges,
+        base_source, top_target, top_source, near_leaves.T, coords,
+        charges.reshape(leaves, M, RHS),
         base_target.T, leaf_basis, leaf_transfer, mid_transfer, base_transfer,
         base_coupling, top_coupling,
     )
-    each = 4
-    return pl.pallas_call(
-        functools.partial(use_kernel, leaves, named),
-        grid=(leaves // each,),
-        out_shape=jax.ShapeDtypeStruct((count, RHS), BF16),
-        in_specs=[SMEM, pl.BlockSpec((each, M, named * M), lambda i: (i, 0, 0)), ANY, ANY, ANY]
-        + [VMEM] * 2,
-        out_specs=pl.BlockSpec((each * M, RHS), lambda i: (i, 0)),
-        scratch_shapes=[
-            pltpu.VMEM((3 * count, RHS), BF16),
-            pltpu.SemaphoreType.DMA((3,)),
-        ],
-        compiler_params=pltpu.CompilerParams(vmem_limit_bytes=60 * 1024 * 1024),
-        cost_estimate=pl.CostEstimate(
-            flops=8_000_000_000, bytes_accessed=66_000_000, transcendentals=0
-        ),
-        name="use",
-    )(near_leaves.T, kernels, before, charges, after, fields, basis)
+    return out
 
 
 def solution(mesh):

time: 101 us -> 86.7 us (0.86)
  the two profiles are of different devices: /device:TPU:0 before, /device:TPU:11 now
where the time goes in v3:
time: 86.7 us; the launch traced here: 86.6 us
  Pallas kernels  83.5 us (96%)
  local copies, waits for them, and re-layouts  3.05 us (4%)
    pallas_call x1, Pallas kernels, per_device(): pl.pallas_call(functools.partial(exchange_kernel, devices, leaves, named,...  83.5 us
    unnamed x1, local copies, waits for them, and re-layouts  3.05 us

profile of v3, /device:TPU:11, one launch (start us, length us, event | category | flops | bytes accessed | tf_op | source)
XLA Modules:
  0.0 86.6 jit_solution(8195453863840564213)
XLA Ops:
  0.0 83.5 %exchange.1 = (bf16[8192,128]{1,0:T(8,128)(2,1)}, bf16[28,128,3456]{2,1,0:T(8,128)(2,1)}) custom-call(s32[189]{0:T(256)} %source_ref.1, s32[8]{0:T(128)} %top_target_ref.1, s32[8]{0:T(128)} %top_source_ref.1, s32[27,64]{1,0:T(8,128)} %bitcast.4, f32[3,8192]{1,0:T(4,128)} %coords_ref.1, bf16[64,128,128]{2,1,0:T(8,128)(2,1)} %bitcast.3, s32[1,189]{1,0:T(1,128)} %bitcast.5, ...), custom_call_target="tpu_custom_call" | custom-call | flops 16000000000 | bytes 70000000 | tf_op jit(solution)/shard_map/exchange/pallas_call | solution.py:559
  83.5 3.0 %copy.15 = bf16[8192,128]{1,0:T(8,128)(2,1)} copy(bf16[8192,128]{1,0:T(8,128)(2,1)} %get-tuple-element.6) | data formatting | bytes 4194304

commit v4 on v3

--- a/solution.py
+++ b/solution.py
@@ -81,13 +81,11 @@
 
 
 def levels_of(devices):
-    half = devices // 2
-    low = 2 ** (int(math.log2(half // 4)) // 2)
-    levels, stride = [], 1
-    for size in (low, half // 4 // low, 4):
-        levels.append((stride, size))
-        stride *= size
-    return levels
+    plane = devices // 8
+    if plane <= 4:
+        return [(1, plane), (plane, 4)]
+    low = 2 ** (int(math.log2(plane)) // 2)
+    return [(1, low), (low, plane // low), (plane, 4)]
 
 
 def exchange_kernel(
@@ -182,6 +180,15 @@
         def _():
             chunk_down(c).start()
 
+    def chunk_left(c):
+        @pl.when(has_after)
+        def _():
+            chunk_up(c).wait_send()
+
+        @pl.when(has_before)
+        def _():
+            chunk_down(c).wait_send()
+
     @pl.when(has_after)
     def _():
         points_up().start()
@@ -385,7 +392,8 @@
         def gather(level=level):
             arrived(gather_copies(level))
             start(gather_copies(level + 1))
-        stages.append((level, gather))
+        stages.append((2 * level + 1, gather))
+    at = 2 * len(levels) + 1
 
     def coupled():
         arrived(gather_copies(len(levels)))
@@ -395,18 +403,19 @@
         arrived(reduce_copies(len(levels)))
         reduced_core()
 
-    stages.append((3, coupled))
-    stages.append((4, lambda: start(reduce_copies(len(levels)))))
-    stages.append((5, core_reduced))
-    at = 6
+    stages.append((at, coupled))
+    stages.append((at + 1, lambda: start(reduce_copies(len(levels)))))
+    stages.append((at + 2, core_reduced))
+    at += 3
+    gap = 2 if len(levels) == 2 else 1
     for level in range(len(levels) - 1, -1, -1):
         stages.append((at, lambda level=level: start(reduce_copies(level))))
         if level:
             def reduce(level=level):
                 arrived(reduce_copies(level))
                 currents[level - 1][...] = reduced(level).astype(BF16)
-            stages.append((at + 1, reduce))
-        at += 2
+            stages.append((at + gap, reduce))
+        at += gap + 1
 
     steps, kept = leaves // EACH, KEEP // EACH
     spilled = steps - kept
@@ -430,9 +439,10 @@
         for when, stage in stages:
             pl.when(i == when)(stage)
 
-        @pl.when((i < 8) | (i % 2 == 1))
-        def _():
-            send_chunk(4 + jnp.where(i < 8, i, 8 + (i - 9) // 2))
+        @pl.when(i < CHUNKS - 4)
+        def _():
+            chunk_left(i + 1)
+            send_chunk(i + 4)
 
         @pl.when(i >= kept)
         def _():
@@ -513,23 +523,16 @@
         sent(gather_copies(level))
         sent(reduce_copies(level))
 
-    def drain_up(c, carry):
-        chunk_up(c).wait_send()
-        return carry
-
-    def drain_down(c, carry):
-        chunk_down(c).wait_send()
-        return carry
+    for c in (0, CHUNKS - 3, CHUNKS - 2, CHUNKS - 1):
+        chunk_left(c)
 
     @pl.when(has_after)
     def _():
         points_up().wait_send()
-        lax.fori_loop(0, CHUNKS, drain_up, 0)
 
     @pl.when(has_before)
     def _():
         points_down().wait_send()
-        lax.fori_loop(0, CHUNKS, drain_down, 0)
 
 
 def per_device(

time: 86.7 us -> 79.9 us (0.922)
  the two profiles are of different devices: /device:TPU:11 before, /device:TPU:0 now
where the time goes in v4:
time: 79.9 us; the launch traced here: 79.2 us
  Pallas kernels  76.1 us (95%)
  local copies, waits for them, and re-layouts  3.05 us (4%)
    pallas_call x1, Pallas kernels, per_device(): pl.pallas_call(functools.partial(exchange_kernel, devices, leaves, named,...  76.1 us
    unnamed x1, local copies, waits for them, and re-layouts  3.05 us

profile of v4, /device:TPU:0, one launch (start us, length us, event | category | flops | bytes accessed | tf_op | source)
XLA Modules:
  0.0 79.2 jit_solution(3784587376378858203)
XLA Ops:
  0.0 76.1 %exchange.1 = (bf16[8192,128]{1,0:T(8,128)(2,1)}, bf16[28,128,3456]{2,1,0:T(8,128)(2,1)}) custom-call(s32[189]{0:T(256)} %source_ref.1, s32[8]{0:T(128)} %top_target_ref.1, s32[8]{0:T(128)} %top_source_ref.1, s32[27,64]{1,0:T(8,128)} %bitcast.4, f32[3,8192]{1,0:T(4,128)} %coords_ref.1, bf16[64,128,128]{2,1,0:T(8,128)(2,1)} %bitcast.3, s32[1,189]{1,0:T(1,128)} %bitcast.5, ...), custom_call_target="tpu_custom_call" | custom-call | flops 16000000000 | bytes 70000000 | tf_op jit(solution)/shard_map/exchange/pallas_call | solution.py:562
  76.1 3.0 %copy.15 = bf16[8192,128]{1,0:T(8,128)(2,1)} copy(bf16[8192,128]{1,0:T(8,128)(2,1)} %get-tuple-element.6) | data formatting | bytes 4194304

commit v5 on v4

--- a/solution.py
+++ b/solution.py
@@ -392,8 +392,8 @@
         def gather(level=level):
             arrived(gather_copies(level))
             start(gather_copies(level + 1))
-        stages.append((2 * level + 1, gather))
-    at = 2 * len(levels) + 1
+        stages.append((2 * level, gather))
+    at = 2 * len(levels)
 
     def coupled():
         arrived(gather_copies(len(levels)))
@@ -407,7 +407,7 @@
     stages.append((at + 1, lambda: start(reduce_copies(len(levels)))))
     stages.append((at + 2, core_reduced))
     at += 3
-    gap = 2 if len(levels) == 2 else 1
+    gap = 1
     for level in range(len(levels) - 1, -1, -1):
         stages.append((at, lambda level=level: start(reduce_copies(level))))
         if level:

time: 79.9 us -> 81.4 us (1.019)
  the two profiles are of different devices: /device:TPU:0 before, /device:TPU:9 now
where the time goes in v5:
time: 81.4 us; the launch traced here: 81.3 us
  Pallas kernels  78.2 us (96%)
  local copies, waits for them, and re-layouts  3.05 us (4%)
    pallas_call x1, Pallas kernels, per_device(): pl.pallas_call(functools.partial(exchange_kernel, devices, leaves, named,...  78.2 us
    unnamed x1, local copies, waits for them, and re-layouts  3.05 us

profile of v5, /device:TPU:9, one launch (start us, length us, event | category | flops | bytes accessed | tf_op | source)
XLA Modules:
  0.0 81.3 jit_solution(4504192973618553419)
XLA Ops:
  0.0 78.2 %exchange.1 = (bf16[8192,128]{1,0:T(8,128)(2,1)}, bf16[28,128,3456]{2,1,0:T(8,128)(2,1)}) custom-call(s32[189]{0:T(256)} %source_ref.1, s32[8]{0:T(128)} %top_target_ref.1, s32[8]{0:T(128)} %top_source_ref.1, s32[27,64]{1,0:T(8,128)} %bitcast.4, f32[3,8192]{1,0:T(4,128)} %coords_ref.1, bf16[64,128,128]{2,1,0:T(8,128)(2,1)} %bitcast.3, s32[1,189]{1,0:T(1,128)} %bitcast.5, ...), custom_call_target="tpu_custom_call" | custom-call | flops 16000000000 | bytes 70000000 | tf_op jit(solution)/shard_map/exchange/pallas_call | solution.py:562
  78.2 3.0 %copy.15 = bf16[8192,128]{1,0:T(8,128)(2,1)} copy(bf16[8192,128]{1,0:T(8,128)(2,1)} %get-tuple-element.6) | data formatting | bytes 4194304
